TPU v7x, 32 devices: a whole 2x2x4 slice. The times are simulated.
32 devices in a mesh: dp: 8 (over z, core), tensor: 4 (over y, x).
Axes of the slice: x: 2, y: 2, z: 4, core: 2. Of those that a mesh axis runs over, the one named last changes fastest.
Arguments:
- tokens: bfloat16 [4096, 2048], P('dp'), may hold values from -6 to 6
- segments: int32 [8, 512], P('dp'), may hold values from 0 to 1, never falling along the last dimension, each value on 1 to 511 neighbouring positions
- expert_ids: int32 [4096, 6], P('dp'), may hold values from 0 to 31, all different within a row; in each aligned block of 512 rows (0 to 511, 512 to 1023, ...) at most 144 rows name the same one
- route_weight: float32 [4096, 6], P('dp'), may hold values from 0.1 to 1
- norm1_gain: bfloat16 [2048], P(('dp', 'tensor')), may hold values from 0.5 to 1.5
- q_weight: bfloat16 [2048, 3072], P('dp', 'tensor'), may hold values from -0.125 to 0.125
- kva_weight: bfloat16 [2048, 576], P(('dp', 'tensor')), may hold values from -0.125 to 0.125
- kv_gain: bfloat16 [512], P(('dp', 'tensor')), may hold values from 0.5 to 1.5
- kvb_weight: bfloat16 [512, 4096], P('dp', 'tensor'), may hold values from -0.25 to 0.25
- out_weight: bfloat16 [2048, 2048], P('tensor', 'dp'), may hold values from -1 to 1
- norm2_gain: bfloat16 [2048], P(('dp', 'tensor')), may hold values from 0.5 to 1.5
- shared_gate: bfloat16 [2048, 2816], P('dp', 'tensor'), may hold values from -0.125 to 0.125
- shared_up: bfloat16 [2048, 2816], P('dp', 'tensor'), may hold values from -0.125 to 0.125
- shared_down: bfloat16 [2816, 2048], P('tensor', 'dp'), may hold values from -0.21875 to 0.21875
- expert_gate: bfloat16 [32, 2048, 1408], P('dp', None, 'tensor'), may hold values from -0.125 to 0.125
- expert_up_projection: bfloat16 [32, 2048, 1408], P('dp', None, 'tensor'), may hold values from -0.125 to 0.125
- expert_down: bfloat16 [32, 1408, 2048], P('dp', 'tensor'), may hold values from -0.3125 to 0.3125
- cotangent: bfloat16 [4096, 2048], P('dp'), may hold values from -6 to 6
Outputs:
- output: bfloat16 [4096, 2048], P('dp')
- grad_tokens: float32 [4096, 2048], P('dp')
- grad_norm1_gain: float32 [2048], P(('dp', 'tensor'))
- grad_q_weight: float32 [2048, 3072], P('dp', 'tensor')
- grad_kva_weight: float32 [2048, 576], P(('dp', 'tensor'))
- grad_kv_gain: float32 [512], P(('dp', 'tensor'))
- grad_kvb_weight: float32 [512, 4096], P('dp', 'tensor')
- grad_out_weight: float32 [2048, 2048], P('tensor', 'dp')
- grad_norm2_gain: float32 [2048], P(('dp', 'tensor'))
- grad_shared_gate: float32 [2048, 2816], P('dp', 'tensor')
- grad_shared_up: float32 [2048, 2816], P('dp', 'tensor')
- grad_shared_down: float32 [2816, 2048], P('tensor', 'dp')
- grad_expert_gate: float32 [32, 2048, 1408], P('dp', None, 'tensor')
- grad_expert_up: float32 [32, 2048, 1408], P('dp', None, 'tensor')
- grad_expert_down: float32 [32, 1408, 2048], P('dp', 'tensor')
Inputs may be any that keep to these rules, and one draw needn't show every extreme that they name: `segments`: each row holds 2 sequences laid end to end; numbers never fall along a row; each sequence has 1 to 511 tokens. `expert_ids`: each token names 6 different experts; among the 512 tokens of one index of dp no expert is named more than 144 times, a bound that some block reaches.
All inputs are finite; a program needn't handle non-finite values.
Results may differ from a plain program's by a relative error of at most 0.025.
Values may be sent and summed in bfloat16 or wider, within the bound.
A program may use at most 384 MiB of HBM per device.

v0:
```python
import functools

import jax
import jax.numpy as jnp
from jax import lax
from jax.experimental import pallas as pl
from jax.experimental.pallas import tpu as pltpu
from jax.sharding import PartitionSpec as P


NOPE = 128
ROPE = 64
VDIM = 128
LATENT = 512
SEGS = 2


DP, TP = "dp", "tensor"
epsilon = 1e-06
theta_base = 10000.0


def dot_last(left, right):
    return lax.dot_general(
        left,
        right,
        (((left.ndim - 1,), (right.ndim - 1,)), ((), ())),
        preferred_element_type=jnp.float32,
    )


def dot_first(left, right):
    return lax.dot_general(
        left, right, (((0,), (0,)), ((), ())), preferred_element_type=jnp.float32
    )


def rotate(vector, cosine, sine_part):
    half_width = vector.shape[-1] // 2
    lower_half = vector[..., :half_width]
    upper_half = vector[..., half_width:]
    return jnp.concatenate(
        [
            lower_half * cosine - upper_half * sine_part,
            upper_half * cosine + lower_half * sine_part,
        ],
        axis=-1,
    )


def angles(segment_row):
    seq_len = segment_row.shape[0]
    member = segment_row[:, None] == jnp.arange(SEGS, dtype=jnp.int32)[None, :]
    seq_sizes = jnp.sum(member.astype(jnp.int32), axis=0)
    starts = jnp.cumsum(seq_sizes) - seq_sizes
    seq_first = jnp.sum(jnp.where(member, starts[None, :], 0), axis=1)
    seq_place = (jnp.arange(seq_len, dtype=jnp.int32) - seq_first).astype(jnp.float32)
    inv_freq = theta_base ** (-2.0 * jnp.arange(ROPE // 2, dtype=jnp.float32) / ROPE)
    angle_all = seq_place[:, None] * inv_freq[None, :]
    return (jnp.cos(angle_all), jnp.sin(angle_all))


def norm_scale(vector):
    return lax.rsqrt(jnp.mean(vector * vector, axis=-1, keepdims=True) + epsilon)


def norm_back(grad_hat, hat_value, inv_root):
    return inv_root * (
        grad_hat - hat_value * jnp.mean(grad_hat * hat_value, axis=-1, keepdims=True)
    )


def swish_derivative(grad_act, gate_act, up_act):
    sigma = jax.nn.sigmoid(gate_act)
    return (
        grad_act * up_act * sigma * (1.0 + gate_act * (1.0 - sigma)),
        grad_act * gate_act * sigma,
    )


def after(value, *earlier):
    if not earlier:
        return value
    return lax.optimization_barrier((value,) + earlier)[0]


def shift_tensor(value, step):
    size = lax.axis_size(TP)
    return lax.ppermute(value, TP, [(i, (i + step) % size) for i in range(size)])


def shift_chips(value, step):
    chips = lax.axis_size(DP) // 2
    pairs = [(2 * z + c, 2 * ((z + step) % chips) + c) for z in range(chips) for c in range(2)]
    return lax.ppermute(value, DP, pairs)


def swap_cores(value):
    return lax.ppermute(value, DP, [(i, i ^ 1) for i in range(lax.axis_size(DP))])


def pick(value, index, axis=0):
    return lax.dynamic_index_in_dim(value, index, axis, keepdims=False)


def place(pieces, owners, hold=()):
    whole = after(jnp.zeros((len(pieces),) + pieces[0].shape, pieces[0].dtype), *hold)
    for piece, owner in zip(pieces, owners):
        whole = lax.dynamic_update_index_in_dim(whole, piece, owner, 0)
    return whole


def gather_dp(value, hold=()):
    ranks = lax.axis_size(DP)
    chips = ranks // 2
    index = lax.axis_index(DP)
    core, chip = index % 2, index // 2
    mine = [value] + [shift_chips(value, k) for k in range(1, chips)]
    other = [swap_cores(piece) for piece in mine]
    origin = [(chip - k) % chips for k in range(chips)]
    owners = [2 * z + core for z in origin] + [2 * z + 1 - core for z in origin]
    return place(mine + other, owners, hold)


def gather_tensor(value):
    size = lax.axis_size(TP)
    index = lax.axis_index(TP)
    pieces = [value] + [shift_tensor(value, j) for j in range(1, size)]
    whole = place(pieces, [(index - j) % size for j in range(size)])
    return whole.reshape((size * value.shape[0],) + value.shape[1:])


def total(pieces):
    whole = pieces[0].astype(jnp.float32)
    for piece in pieces[1:]:
        whole = whole + piece.astype(jnp.float32)
    return whole


def scatter_tensor(value):
    size = lax.axis_size(TP)
    index = lax.axis_index(TP)
    value = value.reshape((size, value.shape[0] // size) + value.shape[1:])
    pieces = [shift_tensor(pick(value, (index + j) % size), j) for j in range(1, size)]
    return total([pick(value, index)] + pieces)


def shift_outer(value, step):
    size = lax.axis_size(TP)
    inner = size // 2
    pairs = [(i, (i + step * inner) % size) for i in range(size)]
    return lax.ppermute(value, TP, pairs)


def shift_inner(value, step):
    size = lax.axis_size(TP)
    inner = size // 2
    pairs = [(i, i // inner * inner + (i + step) % inner) for i in range(size)]
    return lax.ppermute(value, TP, pairs)


def scatter_half(held, inner_first, hold_first, hold_second, hold_last):
    inner = len(held) // 2
    chips, dtype = held[0].shape[0], held[0].dtype
    if inner_first:
        groups = [[held[o * inner + i] for i in range(inner)] for o in range(2)]
        first, second = shift_inner, shift_outer
    else:
        groups = [[held[o * inner + i] for o in range(2)] for i in range(inner)]
        first, second = shift_outer, shift_inner
    moved = [[first(group[n], n) for n in range(1, len(group))] for group in groups]
    sums = [
        total([after(group[0], *hold_first)] + arrived).astype(dtype)
        for group, arrived in zip(groups, moved)
    ]
    moved = [second(sums[n], n) for n in range(1, len(sums))]
    kept = after(sums[0], *hold_second)
    pieces = [total([kept[k]] + [piece[k] for piece in moved]).astype(dtype) for k in range(chips)]
    moved = [shift_chips(pieces[k], k) for k in range(1, chips)]
    return total([after(pieces[0], *hold_last)] + moved)


def scatter_all(held, hold_first=(), hold_second=(), hold_last=()):
    return jnp.concatenate(
        [
            scatter_half(half, n == 0, hold_first, hold_second, hold_last)
            for n, half in enumerate(held)
        ],
        axis=1,
    )


def scatter_small(value, hold):
    ranks, size = lax.axis_size(DP), lax.axis_size(TP)
    index, column = lax.axis_index(DP), lax.axis_index(TP)
    core, chip = index % 2, index // 2
    value = value.reshape(ranks // 2, 2, size, value.shape[-1])
    value = pick(value, core, 1) + swap_cores(pick(value, 1 - core, 1))
    pieces = [shift_tensor(pick(value, (column + j) % size, 1), j) for j in range(1, size)]
    value = total([pick(value, column, 1)] + pieces)
    value = after(value, *hold)
    pieces = [shift_chips(pick(value, (chip + k) % (ranks // 2)), k) for k in range(1, ranks // 2)]
    return total([pick(value, chip)] + pieces)


def slot_tables(ids_all, weights_all, first_expert, local_experts, capacity):
    length = ids_all.shape[2]
    experts = first_expert + jnp.arange(local_experts, dtype=jnp.int32)
    named = ids_all[:, None] == experts[None, :, None, None]
    member = jnp.any(named, axis=2)
    pair_weight = jnp.sum(jnp.where(named, weights_all[:, None], 0.0), axis=2)
    earlier = jnp.arange(length)[:, None] < jnp.arange(length)[None, :]
    rank = jnp.einsum(
        "set,tu->seu",
        member.astype(jnp.bfloat16),
        earlier.astype(jnp.bfloat16),
        preferred_element_type=jnp.float32,
    ).astype(jnp.int32)
    slot = jnp.where(member, rank, -1)
    chosen = slot[:, :, None, :] == jnp.arange(capacity, dtype=jnp.int32)[None, None, :, None]
    slot_weight = jnp.sum(jnp.where(chosen, pair_weight[:, :, None, :], 0.0), axis=3)
    slot_token = jnp.sum(
        jnp.where(chosen, jnp.arange(length, dtype=jnp.int32) + 1, 0), axis=3
    ) - 1
    return slot_token, slot_weight


def fetch_kernel(token_ref, rows_ref, out_ref):
    experts, room = out_ref.shape[:2]
    slots, length = token_ref.shape[0], rows_ref.shape[0]
    position = lax.broadcasted_iota(jnp.int32, (slots, length), 1)
    chosen = (token_ref[...] == position).astype(jnp.bfloat16)
    fetched = jnp.dot(chosen, rows_ref[...], preferred_element_type=jnp.float32)
    fetched = fetched.astype(jnp.bfloat16)
    for e in range(experts):
        out_ref[e] = fetched[e * room : (e + 1) * room]


def fetch_rows(slot_token, rows):
    ranks, experts, room = slot_token.shape
    length, width = rows.shape[1:]
    slots = experts * room
    return pl.pallas_call(
        fetch_kernel,
        grid=(ranks,),
        in_specs=[
            pl.BlockSpec((None, slots, 1), lambda s: (s, 0, 0)),
            pl.BlockSpec((None, length, width), lambda s: (s, 0, 0)),
        ],
        out_specs=pl.BlockSpec((experts, room, width), lambda s: (0, s, 0)),
        out_shape=jax.ShapeDtypeStruct((experts, ranks * room, width), jnp.bfloat16),
        cost_estimate=pl.CostEstimate(
            flops=2 * ranks * slots * length * width,
            bytes_accessed=2 * ranks * (slots + length) * width,
            transcendentals=0,
        ),
        name="fetch_rows",
    )(slot_token.reshape(ranks, slots, 1), rows)


def return_kernel(with_extra, order_ref, start_ref, token_ref, rows_ref, *refs):
    experts, room, width = rows_ref.shape
    extra_ref, refs = (refs[0], refs[1:]) if with_extra else (None, refs)
    size, count = start_ref.shape[0], refs[0].shape[0]
    arrived_refs, out_refs = refs[: -2 * size], refs[-2 * size :]
    rows = rows_ref[...].reshape(experts * room, width)
    position = lax.broadcasted_iota(jnp.int32, (count, experts * room), 0)
    for step in range(size):
        chosen = (token_ref[...] == position + step * count).astype(jnp.bfloat16)
        sums = jnp.dot(chosen, rows, preferred_element_type=jnp.float32)
        if with_extra:
            begin = pl.multiple_of(start_ref[step] * count, count)
            extra = extra_ref[pl.ds(begin, count)].astype(jnp.float32)
            sums = sums + jnp.where(pl.program_id(0) == 0, extra, 0.0)
        for half in range(2):
            part = sums[:, half * (width // 2) : (half + 1) * (width // 2)]
            if arrived_refs:
                part = part + arrived_refs[half * size + step][...].astype(jnp.float32)
            out_refs[half * size + step][...] = part.astype(jnp.bfloat16)


def return_rows(order, starts, slot_token, rows, length, extra=None, arrived=None):
    steps, (ranks, experts, room), width = order.shape[0], slot_token.shape, rows.shape[2]
    size, slots = starts.shape[0], experts * room
    count = length // size
    more = [] if extra is None else [extra]
    more_specs = [] if extra is None else [pl.BlockSpec((length, width), lambda k, o, s: (0, 0))]
    cut_specs = [pl.BlockSpec((None, count, width // 2), lambda k, o, s: (k, 0, 0))] * (2 * size)
    if arrived is not None:
        more = more + list(arrived[0]) + list(arrived[1])
        more_specs = more_specs + cut_specs
    results = pl.pallas_call(
        functools.partial(return_kernel, extra is not None),
        grid_spec=pltpu.PrefetchScalarGridSpec(
            num_scalar_prefetch=2,
            grid=(steps,),
            in_specs=[
                pl.BlockSpec((None, 1, slots), lambda k, o, s: (o[k], 0, 0)),
                pl.BlockSpec((experts, room, width), lambda k, o, s: (0, o[k], 0)),
            ]
            + more_specs,
            out_specs=cut_specs,
        ),
        out_shape=[jax.ShapeDtypeStruct((steps, count, width // 2), jnp.bfloat16)] * (2 * size),
        cost_estimate=pl.CostEstimate(
            flops=2 * steps * slots * length * width,
            bytes_accessed=2 * steps * (slots + 2 * length) * width,
            transcendentals=0,
        ),
        name="return_rows",
    )(order, starts, slot_token.reshape(ranks, 1, slots), rows, *more)
    return results[:size], results[size:]


def expert_kernel(
    rows_ref, grad_ref, weight_ref, slot_ref, back_ref, hidden_ref, scaled_ref, gate_ref, up_ref, both
):
    width = grad_ref.shape[1]
    half = weight_ref.shape[1] // 2

    @pl.when((pl.program_id(0) == 0) & (pl.program_id(1) == 0))
    def _():
        both[...] = jnp.zeros_like(both)

    acts = jnp.dot(rows_ref[...], weight_ref[...], preferred_element_type=jnp.float32)
    gate_act, up_act = acts[:, :width], acts[:, half : half + width]
    sigma = 1.0 / (1.0 + jnp.exp(-gate_act))
    silu = gate_act * sigma
    hidden = (silu * up_act).astype(jnp.bfloat16)
    hidden_ref[...] = hidden
    scaled_ref[...] = (hidden.astype(jnp.float32) * slot_ref[...]).astype(jnp.bfloat16)
    grad = grad_ref[...] * slot_ref[...]
    gate_grad = (grad * up_act * sigma * (1.0 + gate_act * (1.0 - sigma))).astype(jnp.bfloat16)
    up_grad = (grad * silu).astype(jnp.bfloat16)
    gate_ref[...] = gate_grad
    up_ref[...] = up_grad
    both[:, :width] = gate_grad
    both[:, half : half + width] = up_grad
    back_ref[...] = lax.dot_general(
        both[...], weight_ref[...], (((1,), (1,)), ((), ())), preferred_element_type=jnp.float32
    ).astype(jnp.bfloat16)


def expert_pass(rows, grad_hidden, weights, slot_weight):
    experts, slots, width = rows.shape
    hidden = grad_hidden.shape[2]
    share = slots // 2
    row_spec = pl.BlockSpec((None, share, width), lambda e, i: (e, i, 0))
    hidden_spec = pl.BlockSpec((None, share, hidden), lambda e, i: (e, i, 0))
    hidden_shape = jax.ShapeDtypeStruct((experts, slots, hidden), jnp.bfloat16)
    return pl.pallas_call(
        expert_kernel,
        grid=(experts, 2),
        in_specs=[
            row_spec,
            hidden_spec,
            pl.BlockSpec((None,) + weights.shape[1:], lambda e, i: (e, 0, 0)),
            pl.BlockSpec((None, share, 1), lambda e, i: (e, i, 0)),
        ],
        out_specs=[row_spec] + [hidden_spec] * 4,
        out_shape=[jax.ShapeDtypeStruct(rows.shape, jnp.bfloat16)] + [hidden_shape] * 4,
        scratch_shapes=[pltpu.VMEM((share, weights.shape[2]), jnp.bfloat16)],
        cost_estimate=pl.CostEstimate(
            flops=8 * experts * slots * width * hidden,
            bytes_accessed=4 * experts * (slots + hidden) * width,
            transcendentals=experts * slots * hidden,
        ),
        name="expert_pass",
    )(rows, grad_hidden, weights, slot_weight[..., None])


def side_by_side(value, ranks):
    width = value.shape[1]
    value = value.reshape(ranks, 4, -1, width).transpose(0, 2, 1, 3)
    return value.reshape(-1, 4 * width)


def stacked(value, ranks):
    width = value.shape[1] // 4
    value = value.reshape(ranks, -1, 4, width).transpose(0, 2, 1, 3)
    return value.reshape(-1, width)


def local(
    tokens,
    segments,
    expert_ids,
    route_weight,
    norm1_gain,
    q_weight,
    kva_weight,
    kv_gain,
    kvb_weight,
    out_weight,
    norm2_gain,
    shared_gate,
    shared_up,
    shared_down,
    expert_gate,
    expert_up_projection,
    expert_down,
    cotangent,
):
    length = tokens.shape[0]
    model_width = tokens.shape[1]
    groups = lax.axis_size(TP)
    rank_count = lax.axis_size(DP)
    local_experts = expert_gate.shape[0]
    experts_all = local_experts * rank_count
    choose = expert_ids.shape[1]
    capacity = groups * -(-(3 * length * choose) // (2 * experts_all * groups))
    slot_room = 16 * -(-capacity // 16)
    head_count = q_weight.shape[1] // (NOPE + ROPE)
    score_scale = (NOPE + ROPE) ** (-0.5)
    dp_index = lax.axis_index(DP)
    column = lax.axis_index(TP)
    chips = rank_count // 2
    token_share = length // groups

    def quarter(rows):
        return lax.dynamic_slice_in_dim(rows, column * token_share, token_share, 0)

    gain_widths = (norm1_gain.shape[0], kv_gain.shape[0], norm2_gain.shape[0])
    latent_rows, latent_width = kva_weight.shape
    gain_row = jnp.concatenate([norm1_gain, kv_gain, norm2_gain])
    gain_columns = -(-sum(gain_widths) // latent_rows)
    gain_row = jnp.pad(gain_row, (0, gain_columns * latent_rows - sum(gain_widths)))
    small = jnp.concatenate([kva_weight, gain_row.reshape(latent_rows, gain_columns)], axis=1)
    small = gather_dp(small)
    pieces = [small] + [shift_tensor(small, j) for j in range(1, groups)]
    pieces = tuple(pieces)
    small_all = jnp.zeros((rank_count, groups) + small.shape[1:], small.dtype)
    for j, piece in enumerate(pieces):
        small_all = lax.dynamic_update_index_in_dim(small_all, piece, (column - j) % groups, 1)
    small_all = small_all.reshape(-1, latent_width + gain_columns)
    latent_full = small_all[:, :latent_width]
    gains_all = small_all[:, latent_width:].reshape(rank_count * groups, -1).astype(jnp.float32)
    attention_norm_scale = gains_all[:, : gain_widths[0]].reshape(-1)
    latent_norm_scale = gains_all[:, gain_widths[0] : gain_widths[0] + gain_widths[1]].reshape(-1)
    feedforward_norm_scale = gains_all[:, gain_widths[0] + gain_widths[1] : sum(gain_widths)].reshape(-1)

    expand_full = gather_dp(kvb_weight, pieces).reshape(-1, kvb_weight.shape[1])
    query_full = gather_dp(q_weight, pieces).reshape(-1, q_weight.shape[1])
    output_rows = gather_dp(after(out_weight, small_all))
    output_full = output_rows.transpose(1, 0, 2).reshape(out_weight.shape[0], -1)

    routing = jnp.concatenate([expert_ids.astype(jnp.float32).T, route_weight.T], axis=0)
    routing_all = gather_dp(routing)
    ids_all, weights_all = routing_all[:, :choose].astype(jnp.int32), routing_all[:, choose:]
    grad_all = lax.all_gather(
        quarter(cotangent), (DP, TP), axis=0, tiled=True
    )
    residual_stream = tokens.astype(jnp.float32)
    inv_one = norm_scale(residual_stream)
    hat_one = residual_stream * inv_one
    normed_one = (hat_one * attention_norm_scale).astype(jnp.bfloat16)
    segment_row = segments[0]
    cosine, sine_part = angles(segment_row)
    queries = jnp.dot(normed_one, query_full, preferred_element_type=jnp.float32).reshape(
        length, head_count, NOPE + ROPE
    )
    q_rot = jnp.concatenate(
        [
            queries[..., :NOPE],
            rotate(queries[..., NOPE:], cosine[:, None, :], sine_part[:, None, :]),
        ],
        axis=-1,
    ).astype(jnp.bfloat16)
    compressed = jnp.dot(normed_one, latent_full, preferred_element_type=jnp.float32)
    latent_raw = compressed[:, :LATENT]
    inv_kv = norm_scale(latent_raw)
    hat_kv = latent_raw * inv_kv
    latent_low = (hat_kv * latent_norm_scale).astype(jnp.bfloat16)
    key_rot = rotate(compressed[:, LATENT:], cosine, sine_part).astype(jnp.bfloat16)
    keyval = (
        jnp.dot(latent_low, expand_full, preferred_element_type=jnp.float32)
        .astype(jnp.bfloat16)
        .reshape(length, head_count, NOPE + VDIM)
    )
    key_nope = keyval[..., :NOPE]
    values = keyval[..., NOPE:]
    positions = jnp.arange(length, dtype=jnp.int32)
    allowed = (segment_row[:, None] == segment_row[None, :]) & (
        positions[None, :] <= positions[:, None]
    )

    def raw_scores():
        dots = jnp.einsum(
            "thd,shd->hts", q_rot[..., :NOPE], key_nope, preferred_element_type=jnp.float32
        )
        dots = dots + jnp.einsum(
            "thr,sr->hts", q_rot[..., NOPE:], key_rot, preferred_element_type=jnp.float32
        )
        return jnp.where(allowed[None], dots * score_scale, -1000000000.0)

    scores = raw_scores()
    row_peak = jnp.max(scores, axis=-1, keepdims=True)
    log_total = jnp.log(jnp.sum(jnp.exp(scores - row_peak), axis=-1, keepdims=True)) + row_peak
    attn_probs = jnp.exp(scores - log_total)
    mixed_heads = (
        jnp.einsum(
            "hts,shv->thv",
            attn_probs.astype(jnp.bfloat16),
            values,
            preferred_element_type=jnp.float32,
        )
        .astype(jnp.bfloat16)
        .reshape(length, head_count * VDIM)
    )
    attn_out = scatter_tensor(
        jnp.dot(mixed_heads, output_full, preferred_element_type=jnp.float32).astype(jnp.bfloat16)
    )
    middle = quarter(tokens).astype(jnp.float32) + after(attn_out, grad_all)
    inv_two = norm_scale(middle)
    hat_two = middle * inv_two
    normed_two = (hat_two * feedforward_norm_scale).astype(jnp.bfloat16)
    rows_all = lax.all_gather(normed_two, (DP, TP), axis=0, tiled=True)
    feedforward_normed_input = lax.dynamic_slice_in_dim(rows_all, dp_index * length, length, 0)

    gate_lift_full = lax.all_gather(
        jnp.concatenate([shared_gate, shared_up], axis=1), DP, axis=0, tiled=True
    )
    lower_full = lax.all_gather(shared_down, DP, axis=1, tiled=True)

    slot_token, slot_weight = slot_tables(
        ids_all, weights_all, dp_index * local_experts, local_experts, slot_room
    )
    inner = groups // 2
    share = slot_token // token_share
    step = (share // inner - column // inner) % 2 * inner + (share - column) % inner
    outer_steps = jnp.arange(groups, dtype=jnp.int32) // inner
    inner_steps = jnp.arange(groups, dtype=jnp.int32) % inner
    step_starts = (column // inner + outer_steps) % 2 * inner + (column + inner_steps) % inner
    near_token = jnp.where(slot_token < 0, -1, step * token_share + slot_token % token_share)
    slot_weight = slot_weight.transpose(1, 0, 2).reshape(local_experts, -1)
    chip_steps = (dp_index // 2 + jnp.arange(chips, dtype=jnp.int32)) % chips
    own_order = 2 * chip_steps + dp_index % 2
    other_order = 2 * chip_steps + 1 - dp_index % 2
    expert_width = expert_gate.shape[2]
    lane_pad = ((0, 0), (0, 0), (0, -expert_width % 128))
    gate_up = jnp.concatenate(
        [jnp.pad(expert_gate, lane_pad), jnp.pad(expert_up_projection, lane_pad)], axis=2
    )
    grad_arrived = fetch_rows(slot_token, grad_all.reshape(rank_count, length, model_width))
    hidden_state_gradient = jnp.einsum(
        "erd,efd->erf", grad_arrived, expert_down, preferred_element_type=jnp.float32
    )
    received_rows = fetch_rows(slot_token, rows_all.reshape(rank_count, length, model_width))
    grad_inputs, expert_hidden, weighted_hidden, expert_gate_gradient, expert_up_gradient = (
        expert_pass(received_rows, hidden_state_gradient, gate_up, slot_weight)
    )

    def cut_back(rows, extra=None):
        other = return_rows(other_order, step_starts, near_token, rows, length)
        arrived = [[swap_cores(piece) for piece in half] for half in other]
        held = return_rows(
            own_order, step_starts, near_token, rows, length, extra, arrived
        )
        return held, other

    grad_cut, grad_other = cut_back(grad_inputs)
    expert_out = jnp.einsum(
        "erf,efd->erd", after(expert_hidden, grad_other[0][0]), expert_down,
        preferred_element_type=jnp.float32,
    )
    expert_out = (expert_out * slot_weight[..., None]).astype(jnp.bfloat16)
    grad_expert_down = jnp.einsum(
        "erf,erd->efd", weighted_hidden, grad_arrived, preferred_element_type=jnp.float32
    )
    grad_expert_gate = jnp.einsum(
        "erd,erf->edf", received_rows, expert_gate_gradient, preferred_element_type=jnp.float32
    )
    grad_expert_up = jnp.einsum(
        "erd,erf->edf", received_rows, expert_up_gradient, preferred_element_type=jnp.float32
    )

    hidden_width = shared_gate.shape[1]
    gate_lift_act = jnp.dot(
        feedforward_normed_input, gate_lift_full, preferred_element_type=jnp.float32
    )
    shared_gate_act, shared_up_act = gate_lift_act[:, :hidden_width], gate_lift_act[:, hidden_width:]
    shared_hidden = (jax.nn.silu(shared_gate_act) * shared_up_act).astype(jnp.bfloat16)
    shared_out = jnp.dot(shared_hidden, lower_full, preferred_element_type=jnp.float32).astype(
        jnp.bfloat16
    )
    out_cut, out_other = cut_back(expert_out, shared_out)
    block_out = scatter_all(out_cut)
    output_share = (middle + block_out).astype(jnp.bfloat16)
    output = gather_tensor(output_share)
    grad_out = quarter(cotangent).astype(jnp.float32)
    grad_shared_hidden = dot_last(cotangent, lower_full)
    grad_sgate, grad_sup = swish_derivative(grad_shared_hidden, shared_gate_act, shared_up_act)
    grad_gate_lift = jnp.concatenate(
        [grad_sgate.astype(jnp.bfloat16), grad_sup.astype(jnp.bfloat16)], axis=1
    )
    grad_lower = dot_first(shared_hidden, cotangent).astype(jnp.bfloat16)
    grad_gate_lift_full = dot_first(feedforward_normed_input, grad_gate_lift).astype(jnp.bfloat16)
    shared_grad = dot_last(grad_gate_lift, gate_lift_full).astype(jnp.bfloat16)
    shared_grad_share = scatter_tensor(shared_grad)
    routed_grad = scatter_all(
        grad_cut,
        hold_first=(out_other[0][0], shared_grad, grad_gate_lift_full),
        hold_second=(out_cut[0][0], grad_lower),
        hold_last=(grad_expert_down,),
    )
    grad_normed_two = shared_grad_share + routed_grad
    grad_gain_two = jnp.sum(grad_normed_two * hat_two, axis=0)
    grad_middle = grad_out + norm_back(grad_normed_two * feedforward_norm_scale, hat_two, inv_two)
    grad_middle_low = gather_tensor(grad_middle.astype(jnp.bfloat16))
    grad_middle_low = after(grad_middle_low, grad_expert_up)
    grad_output_full = dot_first(mixed_heads, grad_middle_low)
    grad_mixed = dot_last(grad_middle_low, output_full)
    grad_mixed = (
        grad_mixed.astype(jnp.bfloat16)
        .reshape(length, head_count, VDIM)
    )
    scores = raw_scores()
    attn_probs = jnp.exp(scores - log_total)
    grad_probs = jnp.einsum("thv,shv->hts", grad_mixed, values, preferred_element_type=jnp.float32)
    grad_values = jnp.einsum(
        "hts,thv->shv",
        attn_probs.astype(jnp.bfloat16),
        grad_mixed,
        preferred_element_type=jnp.float32,
    )
    row_delta = jnp.sum(attn_probs * grad_probs, axis=-1, keepdims=True)
    grad_scores = (attn_probs * (grad_probs - row_delta)).astype(jnp.bfloat16)
    grad_q_nope = (
        jnp.einsum("hts,shd->thd", grad_scores, key_nope, preferred_element_type=jnp.float32)
        * score_scale
    )
    grad_q_rope = (
        jnp.einsum("hts,sr->thr", grad_scores, key_rot, preferred_element_type=jnp.float32)
        * score_scale
    )
    grad_k_nope = (
        jnp.einsum(
            "hts,thd->shd", grad_scores, q_rot[..., :NOPE], preferred_element_type=jnp.float32
        )
        * score_scale
    )
    grad_k_rope = jnp.einsum(
        "hts,thr->sr", grad_scores, q_rot[..., NOPE:], preferred_element_type=jnp.float32
    )
    grad_k_rope = grad_k_rope * score_scale
    grad_queries = jnp.concatenate(
        [grad_q_nope, rotate(grad_q_rope, cosine[:, None, :], -sine_part[:, None, :])], axis=-1
    )
    grad_queries = grad_queries.astype(jnp.bfloat16).reshape(length, head_count * (NOPE + ROPE))
    grad_keyval = (
        jnp.concatenate([grad_k_nope, grad_values], axis=-1)
        .astype(jnp.bfloat16)
        .reshape(length, head_count * (NOPE + VDIM))
    )
    grad_query_full = dot_first(normed_one, grad_queries)
    grad_expand_full = dot_first(latent_low, grad_keyval)
    grad_latent = dot_last(grad_keyval, expand_full)
    grad_gain_kv = jnp.sum(grad_latent * hat_kv, axis=0)
    grad_latent_raw = norm_back(grad_latent * latent_norm_scale, hat_kv, inv_kv)
    grad_compressed = jnp.concatenate(
        [grad_latent_raw, rotate(grad_k_rope, cosine, -sine_part)], axis=-1
    ).astype(jnp.bfloat16)
    grad_latent_full = dot_first(normed_one, grad_compressed).astype(jnp.bfloat16)
    grad_latent_full = grad_latent_full.reshape((rank_count, groups) + kva_weight.shape)
    latent_parts = [pick(grad_latent_full, column, 1)] + [
        shift_tensor(pick(grad_latent_full, (column + j) % groups, 1), j)
        for j in range(1, groups)
    ]
    grad_normed_one = dot_last(grad_queries, query_full) + dot_last(grad_compressed, latent_full)
    grad_normed_one = grad_normed_one.astype(jnp.bfloat16)
    grad_latent_part = total([after(latent_parts[0], grad_normed_one)] + latent_parts[1:])
    grad_normed_one = scatter_tensor(grad_normed_one)
    hat_one_share = quarter(hat_one)
    grad_gain_one = jnp.sum(grad_normed_one * hat_one_share, axis=0)
    grad_tokens = grad_middle + norm_back(
        grad_normed_one * attention_norm_scale, hat_one_share, quarter(inv_one)
    )
    grad_tokens = gather_tensor(grad_tokens.astype(jnp.bfloat16)).astype(jnp.float32)

    grad_gate_lift_share = lax.psum_scatter(
        grad_gate_lift_full, DP, scatter_dimension=0, tiled=True
    ).astype(jnp.float32)
    grad_shared_gate = grad_gate_lift_share[:, :hidden_width]
    grad_shared_up = grad_gate_lift_share[:, hidden_width:]
    grad_shared_down = lax.psum_scatter(
        grad_lower, DP, scatter_dimension=1, tiled=True
    ).astype(jnp.float32)
    grad_out_weight = lax.psum_scatter(
        grad_output_full.astype(jnp.bfloat16), DP, scatter_dimension=1, tiled=True
    ).astype(jnp.float32)
    query_width, expand_width = 4 * q_weight.shape[1], kvb_weight.shape[1]
    packed_rows = grad_expand_full.shape[0]
    packed_grad = jnp.concatenate(
        [
            side_by_side(grad_query_full.astype(jnp.bfloat16), rank_count),
            grad_expand_full.astype(jnp.bfloat16),
            grad_latent_part.astype(jnp.bfloat16).reshape(packed_rows, -1),
        ],
        axis=1,
    )
    packed_share = lax.psum_scatter(packed_grad, DP, scatter_dimension=0, tiled=True)
    grad_q_weight = stacked(packed_share[:, :query_width], 1).astype(jnp.float32)
    grad_kvb_weight = packed_share[:, query_width : query_width + expand_width].astype(jnp.float32)
    grad_kva_weight = packed_share[:, query_width + expand_width :].astype(jnp.float32)
    grad_kva_weight = grad_kva_weight.reshape(kva_weight.shape)
    gain_grads = jnp.concatenate(
        [
            grad.reshape(rank_count, groups, -1)
            for grad in (grad_gain_one, grad_gain_kv, grad_gain_two)
        ],
        axis=2,
    )
    gain_grads = scatter_small(
        gain_grads, (grad_shared_gate, grad_shared_up, grad_shared_down, grad_out_weight)
    )
    grad_norm1_gain = gain_grads[: gain_widths[0]]
    grad_kv_gain = gain_grads[gain_widths[0] : gain_widths[0] + gain_widths[1]]
    grad_norm2_gain = gain_grads[gain_widths[0] + gain_widths[1] :]
    return (
        output,
        grad_tokens,
        grad_norm1_gain,
        grad_q_weight,
        grad_kva_weight,
        grad_kv_gain,
        grad_kvb_weight,
        grad_out_weight,
        grad_norm2_gain,
        grad_shared_gate,
        grad_shared_up,
        grad_shared_down,
        grad_expert_gate,
        grad_expert_up,
        grad_expert_down,
    )


def solution(mesh):
    in_specs = (
        P(DP, None),
        P(DP, None),
        P(DP, None),
        P(DP, None),
        P((DP, TP)),
        P(DP, TP),
        P((DP, TP), None),
        P((DP, TP)),
        P(DP, TP),
        P(TP, DP),
        P((DP, TP)),
        P(DP, TP),
        P(DP, TP),
        P(TP, DP),
        P(DP, None, TP),
        P(DP, None, TP),
        P(DP, TP, None),
        P(DP, None),
    )
    out_specs = (
        P(DP, None),
        P(DP, None),
        P((DP, TP)),
        P(DP, TP),
        P((DP, TP), None),
        P((DP, TP)),
        P(DP, TP),
        P(TP, DP),
        P((DP, TP)),
        P(DP, TP),
        P(DP, TP),
        P(TP, DP),
        P(DP, None, TP),
        P(DP, None, TP),
        P(DP, TP, None),
    )

    return jax.shard_map(local, mesh=mesh, in_specs=in_specs, out_specs=out_specs, check_vma=False)
```

profile of v0, /device:TPU:0, one launch (start us, length us, event | category | flops | bytes accessed | tf_op | source)
XLA Modules:
  0.0 917.1 jit_solution(6743560509205945846)
XLA Ops:
  31.9 13.1 %collective-permute-done.7 = bf16[8,64,579]{2,1,0:T(8,128)(2,1)S(1)} collective-permute-done((bf16[8,64,579]{2,1,0:T(8,128)(2,1)S(1)}, bf16[8,64,579]{2,1,0:T(8,128)(2,1)S(1)}, u32[]{:S(2)}, u32[]{:S(2)}) %collective-permute-start.7) | collective-permute-done | bytes 592928 | tf_op jit(solution)/shard_map/ppermute | solution.py:89
  47.9 10.4 %collective-permute-done.8 = bf16[8,64,579]{2,1,0:T(8,128)(2,1)S(1)} collective-permute-done((bf16[8,64,579]{2,1,0:T(8,128)(2,1)S(1)}, bf16[8,64,579]{2,1,0:T(8,128)(2,1)S(1)}, u32[]{:S(2)}, u32[]{:S(2)}) %collective-permute-start.8) | collective-permute-done | bytes 592928 | tf_op jit(solution)/shard_map/ppermute | solution.py:89
  58.5 10.4 %collective-permute-start.10 = (bf16[64,1024]{1,0:T(8,128)(2,1)}, bf16[64,1024]{1,0:T(8,128)(2,1)}, u32[]{:S(2)}, u32[]{:S(2)}) collective-permute-start(bf16[64,1024]{1,0:T(8,128)(2,1)} %param.26), channel_id=1, source_target_pairs={{0,8},{4,12},{8,16},{12,20},{16,24},{20,28},{24,0},{28,4},{1,9},{5... | collective-permute-start | bytes 393224 | tf_op jit(solution)/shard_map/ppermute | solution.py:95
  76.4 6.5 collective-permute-start.11
  83.8 10.5 %collective-permute-done.11 = bf16[64,1024]{1,0:T(8,128)(2,1)S(1)} collective-permute-done((bf16[64,1024]{1,0:T(8,128)(2,1)}, bf16[64,1024]{1,0:T(8,128)(2,1)S(1)}, u32[]{:S(2)}, u32[]{:S(2)}) %collective-permute-start.11) | collective-permute-done | bytes 131104 | tf_op jit(solution)/shard_map/ppermute | solution.py:95
  96.0 4.9 collective-permute-done.12
  160.3 11.4 %collective-permute-done.31 = bf16[128,2048]{1,0:T(8,128)(2,1)} collective-permute-done((bf16[128,2048]{1,0:T(8,128)(2,1)}, bf16[128,2048]{1,0:T(8,128)(2,1)}, u32[]{:S(2)}, u32[]{:S(2)}) %collective-permute-start.31) | collective-permute-done | bytes 524320 | tf_op jit(solution)/shard_map/ppermute | solution.py:89
  171.7 11.0 %collective-permute-done.32 = bf16[128,2048]{1,0:T(8,128)(2,1)} collective-permute-done((bf16[128,2048]{1,0:T(8,128)(2,1)S(1)}, bf16[128,2048]{1,0:T(8,128)(2,1)}, u32[]{:S(2)}, u32[]{:S(2)}) %collective-permute-start.32) | collective-permute-done | bytes 524320 | tf_op jit(solution)/shard_map/ppermute | solution.py:89
  188.9 18.8 %collective-permute-start.34 = (f32[12,512]{1,0:T(8,128)S(1)}, f32[12,512]{1,0:T(8,128)S(1)}, u32[]{:S(2)}, u32[]{:S(2)}) collective-permute-start(f32[12,512]{1,0:T(8,128)S(1)} %pad_maximum_fusion.12), channel_id=1, source_target_pairs={{0,8},{4,12},{8,16},{12,20},{16,24},{20,28},{24,0},{28,4},{1,9},{5... | collective-permute-start | bytes 73736 | tf_op jit(solution)/shard_map/ppermute | solution.py:95
  211.3 8.5 copy.204
  219.8 8.4 copy.205
  228.3 10.7 %fusion.3.weight_ref = bf16[4,2048,768]{2,1,0:T(8,128)(2,1)} fusion(bf16[4,2048,352]{2,1,0:T(8,128)(2,1)} %copy.205, bf16[4,2048,352]{2,1,0:T(8,128)(2,1)} %copy.204), kind=kLoop, calls=%fused_computation.6 | loop fusion | flops 50331648 | bytes 24117248 | tf_op jit(solution)/shard_map/concatenate | solution.py:541
  251.2 19.7 %fetch_rows.3 = bf16[4,1152,2048]{2,1,0:T(8,128)(2,1)} custom-call(s32[8,576,1]{2,1,0:T(8,128)} %sub.242.token_ref, bf16[8,512,2048]{2,1,0:T(8,128)(2,1)} %bitcast.328), custom_call_target="tpu_custom_call" | custom-call | flops 9663676416 | bytes 35651584 | tf_op jit(solution)/shard_map/fetch_rows/pallas_call | solution.py:243
  270.9 17.3 %fusion.116.grad_ref = f32[4,1152,352]{2,1,0:T(8,128)} fusion(bf16[4,1152,2048]{2,1,0:T(8,128)(2,1)} %fetch_rows.3, bf16[4,352,2048]{2,1,0:T(8,128)(2,1)} %param.34), kind=kOutput, calls=%fused_computation.354 | convolution fusion | flops 6643777536 | bytes 31129600 | tf_op jit(solution)/shard_map/erd,efd->erf/dot_general | solution.py:545
  288.2 29.7 %all-gather.7.cloned.1.call-done = bf16[4096,2048]{1,0:T(8,128)(2,1)} async-done(((bf16[128,2048]{1,0:T(8,128)(2,1)}), bf16[4096,2048]{1,0:T(8,128)(2,1)}) %all-gather.7.cloned.1.call-update) | async-done | bytes 16777232 | tf_op jit(solution)/shard_map/all_gather | solution.py:517
  317.9 19.3 %fetch_rows.2.rows_ref = bf16[4,1152,2048]{2,1,0:T(8,128)(2,1)} custom-call(s32[8,576,1]{2,1,0:T(8,128)} %sub.242.token_ref, bf16[8,512,2048]{2,1,0:T(8,128)(2,1)} %bitcast.329), custom_call_target="tpu_custom_call" | custom-call | flops 9663676416 | bytes 35651584 | tf_op jit(solution)/shard_map/fetch_rows/pallas_call | solution.py:243
  337.2 43.6 %expert_pass.1 = (bf16[4,1152,2048]{2,1,0:T(8,128)(2,1)}, bf16[4,1152,352]{2,1,0:T(8,128)(2,1)}, bf16[4,1152,352]{2,1,0:T(8,128)(2,1)}, bf16[4,1152,352]{2,1,0:T(8,128)(2,1)}, bf16[4,1152,352]{2,1,0:T(8,128)(2,1)}) custom-call(bf16[4,1152,2048]{2,1,0:T(8,128)(2,1)} %fetch_rows.2.rows_ref, f32[4,1152,352]{2,1,0:T(8,128)} %fusion.116.grad_ref, ...), custom_call_target="tpu_custom_call" | custom-call | flops 26575110144 | bytes 49283072 | tf_op jit(solution)/shard_map/expert_pass/pallas_call | solution.py:351
  380.7 11.2 %return_rows.4 = (bf16[4,128,1024]{2,1,0:T(8,128)(2,1)}, bf16[4,128,1024]{2,1,0:T(8,128)(2,1)}, bf16[4,128,1024]{2,1,0:T(8,128)(2,1)}, bf16[4,128,1024]{2,1,0:T(...) custom-call(s32[4]{0:T(128)} %add_subtract_fusion.order_ref, ...), custom_call_target="tpu_custom_call" | custom-call | flops 4831838208 | bytes 26214400 | tf_op jit(solution)/shard_map/return_rows/pallas_call | solution.py:292
  393.3 17.4 %fusion.rows_ref = bf16[4,1152,2048]{2,1,0:T(8,128)(2,1)} fusion(bf16[4,1152,352]{2,1,0:T(8,128)(2,1)} %get-tuple-element.75, bf16[4,352,2048]{2,1,0:T(8,128)(2,1)} %param.34, f32[4,1152]{1,0:T(4,128)S(1)} %mul.453), kind=kOutput, calls=%fused_computation.1 | convolution fusion | flops 6662651904 | bytes 27904000 | tf_op jit(solution)/shard_map/erf,efd->erd/dot_general | solution.py:562
  410.7 15.2 %fusion.117 = f32[4,352,2048]{2,1,0:T(8,128)} fusion(bf16[4,1152,352]{2,1,0:T(8,128)(2,1)} %get-tuple-element.106, bf16[4,1152,2048]{2,1,0:T(8,128)(2,1)} %fetch_rows.3), kind=kOutput, calls=%fused_computation.355 | convolution fusion | flops 6643777536 | bytes 33652736 | tf_op jit(solution)/shard_map/erf,erd->efd/dot_general | solution.py:567
  425.9 11.2 %return_rows.5 = (bf16[4,128,1024]{2,1,0:T(8,128)(2,1)}, bf16[4,128,1024]{2,1,0:T(8,128)(2,1)}, bf16[4,128,1024]{2,1,0:T(8,128)(2,1)}, bf16[4,128,1024]{2,1,0:T(...) custom-call(s32[4]{0:T(128)} %add_subtract_fusion.order_ref, ...), custom_call_target="tpu_custom_call" | custom-call | flops 4831838208 | bytes 26214400 | tf_op jit(solution)/shard_map/return_rows/pallas_call | solution.py:292
  437.2 8.5 fusion.15
  446.9 6.1 multiply_convert_fusion.3
  458.3 13.0 %return_rows.7 = (bf16[4,128,1024]{2,1,0:T(8,128)(2,1)}, bf16[4,128,1024]{2,1,0:T(8,128)(2,1)}, bf16[4,128,1024]{2,1,0:T(8,128)(2,1)}, bf16[4,128,1024]{2,1,0:T(...) custom-call(s32[4]{0:T(128)} %broadcast_add_fusion.1.order_ref, ...), custom_call_target="tpu_custom_call" | custom-call | flops 4831838208 | bytes 26214400 | tf_op jit(solution)/shard_map/return_rows/pallas_call | solution.py:292
  472.6 6.7 convolution_convert_fusion.7
  480.6 7.6 convolution_convert_fusion
  488.8 5.3 convolution_convert_fusion.5.refs_0_
  510.8 14.1 %return_rows.6 = (bf16[4,128,1024]{2,1,0:T(8,128)(2,1)}, bf16[4,128,1024]{2,1,0:T(8,128)(2,1)}, bf16[4,128,1024]{2,1,0:T(8,128)(2,1)}, bf16[4,128,1024]{2,1,0:T(...) custom-call(s32[4]{0:T(128)} %broadcast_add_fusion.1.order_ref, ...), custom_call_target="tpu_custom_call" | custom-call | flops 4831838208 | bytes 26214400 | tf_op jit(solution)/shard_map/return_rows/pallas_call | solution.py:292
  526.7 4.7 collective-permute-done.81
  533.0 19.2 %collective-permute-done.77 = bf16[4,128,1024]{2,1,0:T(8,128)(2,1)} collective-permute-done((bf16[4,128,1024]{2,1,0:T(8,128)(2,1)}, bf16[4,128,1024]{2,1,0:T(8,128)(2,1)}, u32[]{:S(2)}, u32[]{:S(2)}) %collective-permute-start.77) | collective-permute-done | bytes 1048608 | tf_op jit(solution)/shard_map/ppermute | solution.py:152
  566.5 9.7 %collective-permute-done.79 = bf16[128,1024]{1,0:T(8,128)(2,1)S(1)} collective-permute-done((bf16[128,1024]{1,0:T(8,128)(2,1)S(1)}, bf16[128,1024]{1,0:T(8,128)(2,1)S(1)}, u32[]{:S(2)}, u32[]{:S(2)}) %collective-permute-start.79) | collective-permute-done | bytes 262176 | tf_op jit(solution)/shard_map/ppermute | solution.py:95
  577.8 6.3 collective-permute-start.85
  587.6 9.2 %collective-permute-done.85 = bf16[128,1024]{1,0:T(8,128)(2,1)S(1)} collective-permute-done((bf16[128,1024]{1,0:T(8,128)(2,1)S(1)}, bf16[128,1024]{1,0:T(8,128)(2,1)S(1)}, u32[]{:S(2)}, u32[]{:S(2)}) %collective-permute-start.85) | collective-permute-done | bytes 262176 | tf_op jit(solution)/shard_map/ppermute | solution.py:95
  602.3 15.1 %fusion.118 = f32[4,2048,352]{1,2,0:T(8,128)} fusion(bf16[4,1152,2048]{2,1,0:T(8,128)(2,1)} %fetch_rows.2.rows_ref, bf16[4,1152,352]{2,1,0:T(8,128)(2,1)} %get-tuple-element.116), kind=kOutput, calls=%fused_computation.356 | convolution fusion | flops 6643777536 | bytes 33652736 | tf_op jit(solution)/shard_map/erd,erf->edf/dot_general | solution.py:573
  635.3 22.5 %collective-permute-done.50 = bf16[4,128,1024]{2,1,0:T(8,128)(2,1)} collective-permute-done((bf16[4,128,1024]{2,1,0:T(8,128)(2,1)}, bf16[4,128,1024]{2,1,0:T(8,128)(2,1)}, u32[]{:S(2)}, u32[]{:S(2)}) %collective-permute-start.50) | collective-permute-done | bytes 1048608 | tf_op jit(solution)/shard_map/ppermute | solution.py:159
  668.9 11.3 %collective-permute-done.49 = bf16[4,128,1024]{2,1,0:T(8,128)(2,1)S(1)} collective-permute-done((bf16[4,128,1024]{2,1,0:T(8,128)(2,1)}, bf16[4,128,1024]{2,1,0:T(8,128)(2,1)S(1)}, u32[]{:S(2)}, u32[]{:S(2)}) %collective-permute-start.49) | collective-permute-done | bytes 1048608 | tf_op jit(solution)/shard_map/ppermute | solution.py:159
  680.6 5.3 collective-permute-done.51
  723.9 7.9 collective-permute-start.52
  735.1 6.4 collective-permute-start.54
  758.9 5.3 collective-permute-done.58
  764.2 16.0 %collective-permute-done.59 = bf16[128,1024]{1,0:T(8,128)(2,1)S(1)} collective-permute-done((bf16[128,1024]{1,0:T(8,128)(2,1)S(1)}, bf16[128,1024]{1,0:T(8,128)(2,1)S(1)}, u32[]{:S(2)}, u32[]{:S(2)}) %collective-permute-start.59) | collective-permute-done | bytes 262176 | tf_op jit(solution)/shard_map/ppermute | solution.py:95
  786.3 15.1 %fusion.119 = f32[4,2048,352]{1,2,0:T(8,128)} fusion(bf16[4,1152,2048]{2,1,0:T(8,128)(2,1)} %fetch_rows.2.rows_ref, bf16[4,1152,352]{2,1,0:T(8,128)(2,1)} %get-tuple-element.120), kind=kOutput, calls=%fused_computation.357 | convolution fusion | flops 6643777536 | bytes 33652736 | tf_op jit(solution)/shard_map/erd,erf->edf/dot_general | solution.py:570
  810.6 15.6 %collective-permute-done.62 = bf16[128,2048]{1,0:T(8,128)(2,1)} collective-permute-done((bf16[128,2048]{1,0:T(8,128)(2,1)}, bf16[128,2048]{1,0:T(8,128)(2,1)}, u32[]{:S(2)}, u32[]{:S(2)}) %collective-permute-start.62) | collective-permute-done | bytes 524320 | tf_op jit(solution)/shard_map/ppermute | solution.py:89
  829.2 5.2 collective-permute-done.91
  842.8 12.8 %collective-permute-start.93 = (bf16[128,2048]{1,0:T(8,128)(2,1)S(1)}, bf16[128,2048]{1,0:T(8,128)(2,1)S(1)}, u32[]{:S(2)}, u32[]{:S(2)}) collective-permute-start(bf16[128,2048]{1,0:T(8,128)(2,1)S(1)} %get-tuple-element.203), channel_id=1, source_target_pairs={{0,1},{1,2},{2,3},{3,0},{4,5},{5,6},{6,7},{7,4},{8,9},{9,10},{10,1... | collective-permute-start | bytes 1572872 | tf_op jit(solution)/shard_map/ppermute | solution.py:89
  862.6 6.1 collective-permute-done.97
  871.2 8.7 collective-permute-done.94
  888.2 6.0 collective-permute-start.100
  (609 shorter events, 321.5 us)
Async XLA Ops:
  7.2 177.2 %all-gather.5.cloned.1.call-start = ((), (), s32[]{:S(2)}) async-start(), calls=%async_computation.4 | async-start | bytes 17301504 | tf_op jit(solution)/shard_map/all_gather | solution.py:450
  9.3 308.6 %all-gather.7.cloned.1.call-start = ((), (), s32[]{:S(2)}) async-start(), calls=%async_computation.5 | async-start | bytes 17301504 | tf_op jit(solution)/shard_map/all_gather | solution.py:517
  18.4 88.0 %collective-permute-start.17 = (bf16[256,768]{1,0:T(8,128)(2,1)}, bf16[256,768]{1,0:T(8,128)(2,1)}, u32[]{:S(2)}, u32[]{:S(2)}) collective-permute-start(bf16[256,768]{1,0:T(8,128)(2,1)} %param.23), channel_id=1, source_target_pairs={{0,8},{4,12},{8,16},{12,20},{16,24},{20,28},{24,0},{28,4},{1,9},{5... | collective-permute-start | bytes 1179656 | tf_op jit(solution)/shard_map/ppermute | solution.py:95
  20.2 86.3 %collective-permute-start.18 = (bf16[256,768]{1,0:T(8,128)(2,1)}, bf16[256,768]{1,0:T(8,128)(2,1)}, u32[]{:S(2)}, u32[]{:S(2)}) collective-permute-start(bf16[256,768]{1,0:T(8,128)(2,1)} %param.23), channel_id=1, source_target_pairs={{0,16},{4,20},{8,24},{12,28},{16,0},{20,4},{24,8},{28,12},{1,17},{... | collective-permute-start | bytes 1179656 | tf_op jit(solution)/shard_map/ppermute | solution.py:95
  27.9 30.3 %collective-permute-start.8 = (bf16[8,64,579]{2,1,0:T(8,128)(2,1)S(1)}, bf16[8,64,579]{2,1,0:T(8,128)(2,1)S(1)}, u32[]{:S(2)}, u32[]{:S(2)}) collective-permute-start(bf16[8,64,579]{2,1,0:T(8,128)(2,1)S(1)} %bitcast_dynamic-update-slice_fusion.40), channel_id=1, source_target_pairs={{0,2},{1,3},{2,0},{3,1},{4,6},{5,7},{6,4},{7,5},{8,10},{9,11},{10,... | collective-permute-start | bytes 1778696 | tf_op jit(solution)/shard_map/ppermute | solution.py:89
  30.0 28.5 %collective-permute-start.9 = (bf16[8,64,579]{2,1,0:T(8,128)(2,1)S(1)}, bf16[8,64,579]{2,1,0:T(8,128)(2,1)S(1)}, u32[]{:S(2)}, u32[]{:S(2)}) collective-permute-start(bf16[8,64,579]{2,1,0:T(8,128)(2,1)S(1)} %bitcast_dynamic-update-slice_fusion.40), channel_id=1, source_target_pairs={{0,3},{1,0},{2,1},{3,2},{4,7},{5,4},{6,5},{7,6},{8,11},{9,8},{10,9... | collective-permute-start | bytes 1778696 | tf_op jit(solution)/shard_map/ppermute | solution.py:89
  45.0 61.9 %collective-permute-start.19 = (bf16[256,768]{1,0:T(8,128)(2,1)}, bf16[256,768]{1,0:T(8,128)(2,1)}, u32[]{:S(2)}, u32[]{:S(2)}) collective-permute-start(bf16[256,768]{1,0:T(8,128)(2,1)} %param.23), channel_id=1, source_target_pairs={{0,24},{4,28},{8,0},{12,4},{16,8},{20,12},{24,16},{28,20},{1,25},{... | collective-permute-start | bytes 1179656 | tf_op jit(solution)/shard_map/ppermute | solution.py:95
  58.2 60.0 %collective-permute-start.20 = (bf16[256,768]{1,0:T(8,128)(2,1)}, bf16[256,768]{1,0:T(8,128)(2,1)}, u32[]{:S(2)}, u32[]{:S(2)}) collective-permute-start(bf16[256,768]{1,0:T(8,128)(2,1)} %param.23), channel_id=1, source_target_pairs={{0,4},{4,0},{8,12},{12,8},{16,20},{20,16},{24,28},{28,24},{1,5},{5... | collective-permute-start | bytes 1179656 | tf_op jit(solution)/shard_map/ppermute | solution.py:99
  107.4 33.6 %collective-permute-start.24 = (bf16[512,256]{0,1:T(8,128)(2,1)}, bf16[512,256]{0,1:T(8,128)(2,1)}, u32[]{:S(2)}, u32[]{:S(2)}) collective-permute-start(bf16[512,256]{0,1:T(8,128)(2,1)} %copy.191), channel_id=1, source_target_pairs={{0,8},{4,12},{8,16},{12,20},{16,24},{20,28},{24,0},{28,4},{1,9},{5... | collective-permute-start | bytes 786440 | tf_op jit(solution)/shard_map/ppermute | solution.py:95
  118.3 27.7 %collective-permute-start.25 = (bf16[512,256]{0,1:T(8,128)(2,1)}, bf16[512,256]{0,1:T(8,128)(2,1)}, u32[]{:S(2)}, u32[]{:S(2)}) collective-permute-start(bf16[512,256]{0,1:T(8,128)(2,1)} %copy.191), channel_id=1, source_target_pairs={{0,16},{4,20},{8,24},{12,28},{16,0},{20,4},{24,8},{28,12},{1,17},{... | collective-permute-start | bytes 786440 | tf_op jit(solution)/shard_map/ppermute | solution.py:95
  124.8 26.5 %collective-permute-start.26 = (bf16[512,256]{0,1:T(8,128)(2,1)}, bf16[512,256]{0,1:T(8,128)(2,1)}, u32[]{:S(2)}, u32[]{:S(2)}) collective-permute-start(bf16[512,256]{0,1:T(8,128)(2,1)} %copy.191), channel_id=1, source_target_pairs={{0,24},{4,28},{8,0},{12,4},{16,8},{20,12},{24,16},{28,20},{1,25},{... | collective-permute-start | bytes 786440 | tf_op jit(solution)/shard_map/ppermute | solution.py:95
  126.2 26.1 %collective-permute-start.27 = (bf16[512,256]{0,1:T(8,128)(2,1)}, bf16[512,256]{0,1:T(8,128)(2,1)}, u32[]{:S(2)}, u32[]{:S(2)}) collective-permute-start(bf16[512,256]{0,1:T(8,128)(2,1)} %copy.191), channel_id=1, source_target_pairs={{0,4},{4,0},{8,12},{12,8},{16,20},{20,16},{24,28},{28,24},{1,5},{5... | collective-permute-start | bytes 786440 | tf_op jit(solution)/shard_map/ppermute | solution.py:99
  187.8 249.4 %all-gather.9.cloned.1.call-start = ((), (), s32[]{:S(2)}) async-start(), calls=%async_computation.6 | async-start | bytes 6488064 | tf_op jit(solution)/shard_map/all_gather | solution.py:520
  188.8 258.1 %all-gather.11.cloned.1.call-start = ((), (), s32[]{:S(2)}) async-start(), calls=%async_computation.7 | async-start | bytes 3244032 | tf_op jit(solution)/shard_map/all_gather | solution.py:523
  188.9 50.7 %collective-permute-start.34 = (f32[12,512]{1,0:T(8,128)S(1)}, f32[12,512]{1,0:T(8,128)S(1)}, u32[]{:S(2)}, u32[]{:S(2)}) collective-permute-start(f32[12,512]{1,0:T(8,128)S(1)} %pad_maximum_fusion.12), channel_id=1, source_target_pairs={{0,8},{4,12},{8,16},{12,20},{16,24},{20,28},{24,0},{28,4},{1,9},{5... | collective-permute-start | bytes 73736 | tf_op jit(solution)/shard_map/ppermute | solution.py:95
  207.6 32.4 %collective-permute-start.35 = (f32[12,512]{1,0:T(8,128)S(1)}, f32[12,512]{1,0:T(8,128)S(1)}, u32[]{:S(2)}, u32[]{:S(2)}) collective-permute-start(f32[12,512]{1,0:T(8,128)S(1)} %pad_maximum_fusion.12), channel_id=1, source_target_pairs={{0,16},{4,20},{8,24},{12,28},{16,0},{20,4},{24,8},{28,12},{1,17},{... | collective-permute-start | bytes 73736 | tf_op jit(solution)/shard_map/ppermute | solution.py:95
  207.6 32.5 %collective-permute-start.36 = (f32[12,512]{1,0:T(8,128)S(1)}, f32[12,512]{1,0:T(8,128)S(1)}, u32[]{:S(2)}, u32[]{:S(2)}) collective-permute-start(f32[12,512]{1,0:T(8,128)S(1)} %pad_maximum_fusion.12), channel_id=1, source_target_pairs={{0,24},{4,28},{8,0},{12,4},{16,8},{20,12},{24,16},{28,20},{1,25},{... | collective-permute-start | bytes 73736 | tf_op jit(solution)/shard_map/ppermute | solution.py:95
  210.1 30.8 %collective-permute-start.37 = (f32[12,512]{1,0:T(8,128)S(1)}, f32[12,512]{1,0:T(8,128)S(1)}, u32[]{:S(2)}, u32[]{:S(2)}) collective-permute-start(f32[12,512]{1,0:T(8,128)S(1)} %pad_maximum_fusion.12), channel_id=1, source_target_pairs={{0,4},{4,0},{8,12},{12,8},{16,20},{20,16},{24,28},{28,24},{1,5},{5... | collective-permute-start | bytes 73736 | tf_op jit(solution)/shard_map/ppermute | solution.py:99
  210.1 673.1 %reduce-scatter.7.cloned.1.call-start = ((), (), s32[]{:S(2)}) async-start(), calls=%async_computation.9 | async-start | bytes 3244032 | tf_op jit(solution)/shard_map/reduce_scatter | solution.py:685
  392.0 53.7 %collective-permute-start.67 = (bf16[4,128,1024]{2,1,0:T(8,128)(2,1)}, bf16[4,128,1024]{2,1,0:T(8,128)(2,1)S(1)}, u32[]{:S(2)}, u32[]{:S(2)}) collective-permute-start(bf16[4,128,1024]{2,1,0:T(8,128)(2,1)} %get-tuple-element.74), channel_id=1, source_target_pairs={{0,4},{4,0},{8,12},{12,8},{16,20},{20,16},{24,28},{28,24},{1,5},{5... | collective-permute-start | bytes 3145736 | tf_op jit(solution)/shard_map/ppermute | solution.py:99
  392.3 53.6 %collective-permute-start.68 = (bf16[4,128,1024]{2,1,0:T(8,128)(2,1)}, bf16[4,128,1024]{2,1,0:T(8,128)(2,1)}, u32[]{:S(2)}, u32[]{:S(2)}) collective-permute-start(bf16[4,128,1024]{2,1,0:T(8,128)(2,1)} %get-tuple-element.92), channel_id=1, source_target_pairs={{0,4},{4,0},{8,12},{12,8},{16,20},{20,16},{24,28},{28,24},{1,5},{5... | collective-permute-start | bytes 3145736 | tf_op jit(solution)/shard_map/ppermute | solution.py:99
  392.5 53.7 %collective-permute-start.69 = (bf16[4,128,1024]{2,1,0:T(8,128)(2,1)}, bf16[4,128,1024]{2,1,0:T(8,128)(2,1)}, u32[]{:S(2)}, u32[]{:S(2)}) collective-permute-start(bf16[4,128,1024]{2,1,0:T(8,128)(2,1)} %get-tuple-element.93), channel_id=1, source_target_pairs={{0,4},{4,0},{8,12},{12,8},{16,20},{20,16},{24,28},{28,24},{1,5},{5... | collective-permute-start | bytes 3145736 | tf_op jit(solution)/shard_map/ppermute | solution.py:99
  392.8 53.6 %collective-permute-start.70 = (bf16[4,128,1024]{2,1,0:T(8,128)(2,1)}, bf16[4,128,1024]{2,1,0:T(8,128)(2,1)}, u32[]{:S(2)}, u32[]{:S(2)}) collective-permute-start(bf16[4,128,1024]{2,1,0:T(8,128)(2,1)} %get-tuple-element.94), channel_id=1, source_target_pairs={{0,4},{4,0},{8,12},{12,8},{16,20},{20,16},{24,28},{28,24},{1,5},{5... | collective-permute-start | bytes 3145736 | tf_op jit(solution)/shard_map/ppermute | solution.py:99
  393.0 64.2 %collective-permute-start.71 = (bf16[4,128,1024]{2,1,0:T(8,128)(2,1)}, bf16[4,128,1024]{2,1,0:T(8,128)(2,1)}, u32[]{:S(2)}, u32[]{:S(2)}) collective-permute-start(bf16[4,128,1024]{2,1,0:T(8,128)(2,1)} %get-tuple-element.95), channel_id=1, source_target_pairs={{0,4},{4,0},{8,12},{12,8},{16,20},{20,16},{24,28},{28,24},{1,5},{5... | collective-permute-start | bytes 3145736 | tf_op jit(solution)/shard_map/ppermute | solution.py:99
  457.1 427.9 %reduce-scatter.9.cloned.1.call-start = ((), (), s32[]{:S(2)}) async-start(), calls=%async_computation.10 | async-start | bytes 2359296 | tf_op jit(solution)/shard_map/reduce_scatter | solution.py:688
  457.6 30.6 %collective-permute-start.43 = (bf16[4,128,1024]{2,1,0:T(8,128)(2,1)}, bf16[4,128,1024]{2,1,0:T(8,128)(2,1)}, u32[]{:S(2)}, u32[]{:S(2)}) collective-permute-start(bf16[4,128,1024]{2,1,0:T(8,128)(2,1)} %get-tuple-element.78), channel_id=1, source_target_pairs={{0,4},{4,0},{8,12},{12,8},{16,20},{20,16},{24,28},{28,24},{1,5},{5... | collective-permute-start | bytes 3145736 | tf_op jit(solution)/shard_map/ppermute | solution.py:99
  457.8 30.5 %collective-permute-start.44 = (bf16[4,128,1024]{2,1,0:T(8,128)(2,1)}, bf16[4,128,1024]{2,1,0:T(8,128)(2,1)}, u32[]{:S(2)}, u32[]{:S(2)}) collective-permute-start(bf16[4,128,1024]{2,1,0:T(8,128)(2,1)} %get-tuple-element.79), channel_id=1, source_target_pairs={{0,4},{4,0},{8,12},{12,8},{16,20},{20,16},{24,28},{28,24},{1,5},{5... | collective-permute-start | bytes 3145736 | tf_op jit(solution)/shard_map/ppermute | solution.py:99
  458.1 30.6 %collective-permute-start.45 = (bf16[4,128,1024]{2,1,0:T(8,128)(2,1)}, bf16[4,128,1024]{2,1,0:T(8,128)(2,1)}, u32[]{:S(2)}, u32[]{:S(2)}) collective-permute-start(bf16[4,128,1024]{2,1,0:T(8,128)(2,1)} %get-tuple-element.80), channel_id=1, source_target_pairs={{0,4},{4,0},{8,12},{12,8},{16,20},{20,16},{24,28},{28,24},{1,5},{5... | collective-permute-start | bytes 3145736 | tf_op jit(solution)/shard_map/ppermute | solution.py:99
  497.2 27.8 %collective-permute-start.75 = (bf16[4,128,1024]{2,1,0:T(8,128)(2,1)}, bf16[4,128,1024]{2,1,0:T(8,128)(2,1)}, u32[]{:S(2)}, u32[]{:S(2)}) collective-permute-start(bf16[4,128,1024]{2,1,0:T(8,128)(2,1)} %get-tuple-element.101), channel_id=1, source_target_pairs={{0,1},{1,0},{2,3},{3,2},{4,5},{5,4},{6,7},{7,6},{8,9},{9,8},{10,11... | collective-permute-start | bytes 3145736 | tf_op jit(solution)/shard_map/ppermute | solution.py:159
  505.0 26.3 %collective-permute-start.81 = (bf16[4,128,1024]{2,1,0:T(8,128)(2,1)}, bf16[4,128,1024]{2,1,0:T(8,128)(2,1)}, u32[]{:S(2)}, u32[]{:S(2)}) collective-permute-start(bf16[4,128,1024]{2,1,0:T(8,128)(2,1)} %get-tuple-element.110), channel_id=1, source_target_pairs={{0,2},{1,3},{2,0},{3,1},{4,6},{5,7},{6,4},{7,5},{8,10},{9,11},{10,... | collective-permute-start | bytes 3145736 | tf_op jit(solution)/shard_map/ppermute | solution.py:152
  509.0 43.2 %collective-permute-start.77 = (bf16[4,128,1024]{2,1,0:T(8,128)(2,1)}, bf16[4,128,1024]{2,1,0:T(8,128)(2,1)}, u32[]{:S(2)}, u32[]{:S(2)}) collective-permute-start(bf16[4,128,1024]{2,1,0:T(8,128)(2,1)} %add_convert_fusion.3), channel_id=1, source_target_pairs={{0,2},{1,3},{2,0},{3,1},{4,6},{5,7},{6,4},{7,5},{8,10},{9,11},{10,... | collective-permute-start | bytes 3145736 | tf_op jit(solution)/shard_map/ppermute | solution.py:152
  509.7 48.1 %collective-permute-start.83 = (bf16[4,128,1024]{2,1,0:T(8,128)(2,1)}, bf16[4,128,1024]{2,1,0:T(8,128)(2,1)}, u32[]{:S(2)}, u32[]{:S(2)}) collective-permute-start(bf16[4,128,1024]{2,1,0:T(8,128)(2,1)} %add_convert_fusion.1), channel_id=1, source_target_pairs={{0,1},{1,0},{2,3},{3,2},{4,5},{5,4},{6,7},{7,6},{8,9},{9,8},{10,11... | collective-permute-start | bytes 3145736 | tf_op jit(solution)/shard_map/ppermute | solution.py:159
  560.0 37.0 %collective-permute-start.64 = (bf16[128,2048]{1,0:T(8,128)(2,1)S(1)}, bf16[128,2048]{1,0:T(8,128)(2,1)S(1)}, u32[]{:S(2)}, u32[]{:S(2)}) collective-permute-start(bf16[128,2048]{1,0:T(8,128)(2,1)S(1)} %get-tuple-element.224), channel_id=1, source_target_pairs={{0,1},{1,2},{2,3},{3,0},{4,5},{5,6},{6,7},{7,4},{8,9},{9,10},{10,1... | collective-permute-start | bytes 1572872 | tf_op jit(solution)/shard_map/ppermute | solution.py:89
  564.9 32.1 %collective-permute-start.65 = (bf16[128,2048]{1,0:T(8,128)(2,1)S(1)}, bf16[128,2048]{1,0:T(8,128)(2,1)S(1)}, u32[]{:S(2)}, u32[]{:S(2)}) collective-permute-start(bf16[128,2048]{1,0:T(8,128)(2,1)S(1)} %get-tuple-element.226), channel_id=1, source_target_pairs={{0,2},{1,3},{2,0},{3,1},{4,6},{5,7},{6,4},{7,5},{8,10},{9,11},{10,... | collective-permute-start | bytes 1572872 | tf_op jit(solution)/shard_map/ppermute | solution.py:89
  630.2 256.6 %reduce-scatter.5.cloned.1.call-start = ((), (), s32[]{:S(2)}) async-start(), calls=%async_computation.8 | async-start | bytes 6488064 | tf_op jit(solution)/shard_map/reduce_scatter | solution.py:680
  631.0 273.1 %reduce-scatter.11.cloned.1.call-start = ((), (), s32[]{:S(2)}) async-start(), calls=%async_computation.11 | async-start | bytes 5455872 | tf_op jit(solution)/shard_map/reduce_scatter | solution.py:701
  631.2 26.6 %collective-permute-start.50 = (bf16[4,128,1024]{2,1,0:T(8,128)(2,1)}, bf16[4,128,1024]{2,1,0:T(8,128)(2,1)}, u32[]{:S(2)}, u32[]{:S(2)}) collective-permute-start(bf16[4,128,1024]{2,1,0:T(8,128)(2,1)} %get-tuple-element.87), channel_id=1, source_target_pairs={{0,1},{1,0},{2,3},{3,2},{4,5},{5,4},{6,7},{7,6},{8,9},{9,8},{10,11... | collective-permute-start | bytes 3145736 | tf_op jit(solution)/shard_map/ppermute | solution.py:159
  633.5 30.8 %collective-permute-start.56 = (bf16[4,128,1024]{2,1,0:T(8,128)(2,1)}, bf16[4,128,1024]{2,1,0:T(8,128)(2,1)}, u32[]{:S(2)}, u32[]{:S(2)}) collective-permute-start(bf16[4,128,1024]{2,1,0:T(8,128)(2,1)} %get-tuple-element.91), channel_id=1, source_target_pairs={{0,2},{1,3},{2,0},{3,1},{4,6},{5,7},{6,4},{7,5},{8,10},{9,11},{10,... | collective-permute-start | bytes 3145736 | tf_op jit(solution)/shard_map/ppermute | solution.py:152
  635.2 45.0 %collective-permute-start.49 = (bf16[4,128,1024]{2,1,0:T(8,128)(2,1)}, bf16[4,128,1024]{2,1,0:T(8,128)(2,1)S(1)}, u32[]{:S(2)}, u32[]{:S(2)}) collective-permute-start(bf16[4,128,1024]{2,1,0:T(8,128)(2,1)} %get-tuple-element.85), channel_id=1, source_target_pairs={{0,1},{1,0},{2,3},{3,2},{4,5},{5,4},{6,7},{7,6},{8,9},{9,8},{10,11... | collective-permute-start | bytes 3145736 | tf_op jit(solution)/shard_map/ppermute | solution.py:159
  659.8 26.1 %collective-permute-start.51 = (bf16[4,128,1024]{2,1,0:T(8,128)(2,1)S(1)}, bf16[4,128,1024]{2,1,0:T(8,128)(2,1)S(1)}, u32[]{:S(2)}, u32[]{:S(2)}) collective-permute-start(bf16[4,128,1024]{2,1,0:T(8,128)(2,1)S(1)} %add_convert_fusion.7), channel_id=1, source_target_pairs={{0,2},{1,3},{2,0},{3,1},{4,6},{5,7},{6,4},{7,5},{8,10},{9,11},{10,... | collective-permute-start | bytes 3145736 | tf_op jit(solution)/shard_map/ppermute | solution.py:152
  663.9 80.5 %collective-permute-start.55 = (bf16[4,128,1024]{2,1,0:T(8,128)(2,1)}, bf16[4,128,1024]{2,1,0:T(8,128)(2,1)}, u32[]{:S(2)}, u32[]{:S(2)}) collective-permute-start(bf16[4,128,1024]{2,1,0:T(8,128)(2,1)} %get-tuple-element.89), channel_id=1, source_target_pairs={{0,2},{1,3},{2,0},{3,1},{4,6},{5,7},{6,4},{7,5},{8,10},{9,11},{10,... | collective-permute-start | bytes 3145736 | tf_op jit(solution)/shard_map/ppermute | solution.py:152
  666.9 79.5 %collective-permute-start.57 = (bf16[4,128,1024]{2,1,0:T(8,128)(2,1)}, bf16[4,128,1024]{2,1,0:T(8,128)(2,1)}, u32[]{:S(2)}, u32[]{:S(2)}) collective-permute-start(bf16[4,128,1024]{2,1,0:T(8,128)(2,1)} %add_convert_fusion.5), channel_id=1, source_target_pairs={{0,1},{1,0},{2,3},{3,2},{4,5},{5,4},{6,7},{7,6},{8,9},{9,8},{10,11... | collective-permute-start | bytes 3145736 | tf_op jit(solution)/shard_map/ppermute | solution.py:159
  748.4 31.7 %collective-permute-start.59 = (bf16[128,1024]{1,0:T(8,128)(2,1)S(1)}, bf16[128,1024]{1,0:T(8,128)(2,1)S(1)}, u32[]{:S(2)}, u32[]{:S(2)}) collective-permute-start(bf16[128,1024]{1,0:T(8,128)(2,1)S(1)} %get-tuple-element.240), channel_id=1, source_target_pairs={{0,16},{4,20},{8,24},{12,28},{16,0},{20,4},{24,8},{28,12},{1,17},{... | collective-permute-start | bytes 786440 | tf_op jit(solution)/shard_map/ppermute | solution.py:95
  749.9 30.2 %collective-permute-start.60 = (bf16[128,1024]{1,0:T(8,128)(2,1)S(1)}, bf16[128,1024]{1,0:T(8,128)(2,1)S(1)}, u32[]{:S(2)}, u32[]{:S(2)}) collective-permute-start(bf16[128,1024]{1,0:T(8,128)(2,1)S(1)} %get-tuple-element.239), channel_id=1, source_target_pairs={{0,24},{4,28},{8,0},{12,4},{16,8},{20,12},{24,16},{28,20},{1,25},{... | collective-permute-start | bytes 786440 | tf_op jit(solution)/shard_map/ppermute | solution.py:95
  803.0 56.4 %collective-permute-start.63 = (bf16[128,2048]{1,0:T(8,128)(2,1)}, bf16[128,2048]{1,0:T(8,128)(2,1)}, u32[]{:S(2)}, u32[]{:S(2)}) collective-permute-start(bf16[128,2048]{1,0:T(8,128)(2,1)} %get-tuple-element.209), channel_id=1, source_target_pairs={{0,3},{1,0},{2,1},{3,2},{4,7},{5,4},{6,5},{7,6},{8,11},{9,8},{10,9... | collective-permute-start | bytes 1572872 | tf_op jit(solution)/shard_map/ppermute | solution.py:89
  806.3 28.1 %collective-permute-start.91 = (bf16[128,2048]{1,0:T(8,128)(2,1)}, bf16[128,2048]{1,0:T(8,128)(2,1)S(1)}, u32[]{:S(2)}, u32[]{:S(2)}) collective-permute-start(bf16[128,2048]{1,0:T(8,128)(2,1)} %get-tuple-element.223), channel_id=1, source_target_pairs={{0,2},{1,3},{2,0},{3,1},{4,6},{5,7},{6,4},{7,5},{8,10},{9,11},{10,... | collective-permute-start | bytes 1572872 | tf_op jit(solution)/shard_map/ppermute | solution.py:89
  806.8 29.1 %collective-permute-start.92 = (bf16[128,2048]{1,0:T(8,128)(2,1)}, bf16[128,2048]{1,0:T(8,128)(2,1)}, u32[]{:S(2)}, u32[]{:S(2)}) collective-permute-start(bf16[128,2048]{1,0:T(8,128)(2,1)} %get-tuple-element.222), channel_id=1, source_target_pairs={{0,3},{1,0},{2,1},{3,2},{4,7},{5,4},{6,5},{7,6},{8,11},{9,8},{10,9... | collective-permute-start | bytes 1572872 | tf_op jit(solution)/shard_map/ppermute | solution.py:89
  842.8 27.5 %collective-permute-start.93 = (bf16[128,2048]{1,0:T(8,128)(2,1)S(1)}, bf16[128,2048]{1,0:T(8,128)(2,1)S(1)}, u32[]{:S(2)}, u32[]{:S(2)}) collective-permute-start(bf16[128,2048]{1,0:T(8,128)(2,1)S(1)} %get-tuple-element.203), channel_id=1, source_target_pairs={{0,1},{1,2},{2,3},{3,0},{4,5},{5,6},{6,7},{7,4},{8,9},{9,10},{10,1... | collective-permute-start | bytes 1572872 | tf_op jit(solution)/shard_map/ppermute | solution.py:89
  (160 other events, 1940.1 us)
Sparse Core Ops, SparseCore 0:
  11.5 168.9 all-gather.4
  187.9 129.9 all-gather.6
  320.1 59.0 all-gather.8
  380.6 35.2 all-gather.10
  457.2 37.2 reduce-scatter.6
  630.3 45.0 reduce-scatter.8
  677.8 71.0 reduce-scatter.4
  751.2 81.8 reduce-scatter.10
where the time goes:
time: 929 us; the launch traced here: 917 us
  waiting for transfers between devices  266 us (29%)
  starting transfers between devices  179 us (19%)
  matrix products  149 us (16%)
  Pallas kernels  132 us (14%)
  local copies, waits for them, and re-layouts  94.7 us (10%)
  other arithmetic  79.7 us (9%)
  between operations  16.7 us (2%)
    ppermute x30, starting transfers between devices, shift_chips(): return lax.ppermute(value, DP, pairs)  104 us
    ppermute x27, waiting for transfers between devices, shift_tensor(): lax.ppermute(value, TP, [(i, (i + step) % size) for i in range(size)])  90.1 us
    ppermute x30, waiting for transfers between devices, shift_chips(): return lax.ppermute(value, DP, pairs)  71 us
    ppermute x27, starting transfers between devices, shift_tensor(): lax.ppermute(value, TP, [(i, (i + step) % size) for i in range(size)])  50.9 us
    pallas_call x4, Pallas kernels, return_rows(): pl.pallas_call(functools.partial(return_kernel, extra is not None), grid_...  49.5 us
    pallas_call x1, Pallas kernels, expert_pass(): pl.pallas_call(expert_kernel, grid=(experts, 2), in_specs=[row_spec, hidd...  43.6 us
    pallas_call x2, Pallas kernels, fetch_rows(): pl.pallas_call(fetch_kernel, grid=(ranks,), in_specs=[pl.BlockSpec((None,...  39 us
    ppermute x6, waiting for transfers between devices, shift_inner(): return lax.ppermute(value, TP, pairs)  36.9 us
  transfers between devices with their start and end apart: 114, of which 39 were waited for; matrix products, arithmetic and copies ran while one was open for 33% of the time, Pallas kernels for 14%

commit v1 on v0

--- a/solution.py
+++ b/solution.py
@@ -448,7 +448,7 @@
     routing_all = gather_dp(routing)
     ids_all, weights_all = routing_all[:, :choose].astype(jnp.int32), routing_all[:, choose:]
     grad_all = lax.all_gather(
-        quarter(cotangent), (DP, TP), axis=0, tiled=True
+        after(quarter(cotangent), small), (DP, TP), axis=0, tiled=True
     )
     residual_stream = tokens.astype(jnp.float32)
     inv_one = norm_scale(residual_stream)
@@ -601,13 +601,12 @@
         grad_cut,
         hold_first=(out_other[0][0], shared_grad, grad_gate_lift_full),
         hold_second=(out_cut[0][0], grad_lower),
-        hold_last=(grad_expert_down,),
+        hold_last=(grad_expert_down, grad_expert_gate, grad_expert_up),
     )
     grad_normed_two = shared_grad_share + routed_grad
     grad_gain_two = jnp.sum(grad_normed_two * hat_two, axis=0)
     grad_middle = grad_out + norm_back(grad_normed_two * feedforward_norm_scale, hat_two, inv_two)
     grad_middle_low = gather_tensor(grad_middle.astype(jnp.bfloat16))
-    grad_middle_low = after(grad_middle_low, grad_expert_up)
     grad_output_full = dot_first(mixed_heads, grad_middle_low)
     grad_mixed = dot_last(grad_middle_low, output_full)
     grad_mixed = (
@@ -666,7 +665,8 @@
         shift_tensor(pick(grad_latent_full, (column + j) % groups, 1), j)
         for j in range(1, groups)
     ]
-    grad_normed_one = dot_last(grad_queries, query_full) + dot_last(grad_compressed, latent_full)
+    grad_normed_one = dot_last(grad_queries, query_full)
+    grad_normed_one = grad_normed_one + dot_last(grad_compressed, latent_full)
     grad_normed_one = grad_normed_one.astype(jnp.bfloat16)
     grad_latent_part = total([after(latent_parts[0], grad_normed_one)] + latent_parts[1:])
     grad_normed_one = scatter_tensor(grad_normed_one)

time: 929 us -> 991 us (1.067)
  waiting for transfers between devices: 266 us -> 356 us
  starting transfers between devices: 179 us -> 153 us
    ppermute x27, waiting for transfers between devices: 90.1 us -> 131 us  [shift_tensor(): lax.ppermute(value, TP, [(i, (i + step) % size) for i in range(size)])]
    ppermute x30, waiting for transfers between devices: 71 us -> 103 us  [shift_chips(): return lax.ppermute(value, DP, pairs)]
    ppermute x6, waiting for transfers between devices: 33.2 us -> 61.1 us  [shift_outer(): return lax.ppermute(value, TP, pairs)]
    ppermute x30, starting transfers between devices: 104 us -> 90.4 us  [shift_chips(): return lax.ppermute(value, DP, pairs)]
    ppermute x27, starting transfers between devices: 50.9 us -> 38.5 us  [shift_tensor(): lax.ppermute(value, TP, [(i, (i + step) % size) for i in range(size)])]
    ppermute x6, waiting for transfers between devices: 36.9 us -> 26.6 us  [shift_inner(): return lax.ppermute(value, TP, pairs)]
    unnamed x197 -> x185, local copies, waits for them, and re-layouts: 32.3 us -> 32 us
  transfers between devices with their start and end apart: 114 -> 114, of which waited for: 39 -> 46; matrix products, arithmetic and copies ran while one was open for 33% -> 31% of each run, Pallas kernels for 14% -> 14%
where the time goes in v1:
time: 991 us; the launch traced here: 979 us
  waiting for transfers between devices  356 us (36%)
  starting transfers between devices  153 us (15%)
  matrix products  150 us (15%)
  Pallas kernels  132 us (13%)
  local copies, waits for them, and re-layouts  92.9 us (9%)
  other arithmetic  78 us (8%)
  between operations  16.7 us (2%)
    ppermute x27, waiting for transfers between devices, shift_tensor(): lax.ppermute(value, TP, [(i, (i + step) % size) for i in range(size)])  131 us
    ppermute x30, waiting for transfers between devices, shift_chips(): return lax.ppermute(value, DP, pairs)  103 us
    ppermute x30, starting transfers between devices, shift_chips(): return lax.ppermute(value, DP, pairs)  90.4 us
    ppermute x6, waiting for transfers between devices, shift_outer(): return lax.ppermute(value, TP, pairs)  61.1 us
    pallas_call x4, Pallas kernels, return_rows(): pl.pallas_call(functools.partial(return_kernel, extra is not None), grid_...  49.6 us
    pallas_call x1, Pallas kernels, expert_pass(): pl.pallas_call(expert_kernel, grid=(experts, 2), in_specs=[row_spec, hidd...  43.5 us
    pallas_call x2, Pallas kernels, fetch_rows(): pl.pallas_call(fetch_kernel, grid=(ranks,), in_specs=[pl.BlockSpec((None,...  39.1 us
    ppermute x27, starting transfers between devices, shift_tensor(): lax.ppermute(value, TP, [(i, (i + step) % size) for i in range(size)])  38.5 us
  transfers between devices with their start and end apart: 114, of which 46 were waited for; matrix products, arithmetic and copies ran while one was open for 31% of the time, Pallas kernels for 14%

profile of v1, /device:TPU:0, one launch (start us, length us, event | category | flops | bytes accessed | tf_op | source)
XLA Modules:
  0.0 979.0 jit_solution(7837358856472695050)
XLA Ops:
  32.8 16.9 %collective-permute-done.7 = bf16[8,64,579]{2,1,0:T(8,128)(2,1)S(1)} collective-permute-done((bf16[8,64,579]{2,1,0:T(8,128)(2,1)S(1)}, bf16[8,64,579]{2,1,0:T(8,128)(2,1)S(1)}, u32[]{:S(2)}, u32[]{:S(2)}) %collective-permute-start.7) | collective-permute-done | bytes 592928 | tf_op jit(solution)/shard_map/ppermute | solution.py:89
  50.7 11.8 %collective-permute-done.8 = bf16[8,64,579]{2,1,0:T(8,128)(2,1)S(1)} collective-permute-done((bf16[8,64,579]{2,1,0:T(8,128)(2,1)S(1)}, bf16[8,64,579]{2,1,0:T(8,128)(2,1)S(1)}, u32[]{:S(2)}, u32[]{:S(2)}) %collective-permute-start.8) | collective-permute-done | bytes 592928 | tf_op jit(solution)/shard_map/ppermute | solution.py:89
  76.0 10.9 %collective-permute-done.11 = bf16[64,1024]{1,0:T(8,128)(2,1)S(1)} collective-permute-done((bf16[64,1024]{1,0:T(8,128)(2,1)}, bf16[64,1024]{1,0:T(8,128)(2,1)S(1)}, u32[]{:S(2)}, u32[]{:S(2)}) %collective-permute-start.11) | collective-permute-done | bytes 131104 | tf_op jit(solution)/shard_map/ppermute | solution.py:95
  86.9 7.0 collective-permute-start.12
  93.9 6.2 collective-permute-done.12
  160.2 11.6 %collective-permute-done.31 = bf16[128,2048]{1,0:T(8,128)(2,1)} collective-permute-done((bf16[128,2048]{1,0:T(8,128)(2,1)}, bf16[128,2048]{1,0:T(8,128)(2,1)}, u32[]{:S(2)}, u32[]{:S(2)}) %collective-permute-start.31) | collective-permute-done | bytes 524320 | tf_op jit(solution)/shard_map/ppermute | solution.py:89
  171.8 10.5 %collective-permute-done.32 = bf16[128,2048]{1,0:T(8,128)(2,1)} collective-permute-done((bf16[128,2048]{1,0:T(8,128)(2,1)S(1)}, bf16[128,2048]{1,0:T(8,128)(2,1)}, u32[]{:S(2)}, u32[]{:S(2)}) %collective-permute-start.32) | collective-permute-done | bytes 524320 | tf_op jit(solution)/shard_map/ppermute | solution.py:89
  188.8 16.4 %collective-permute-start.34 = (f32[12,512]{1,0:T(8,128)S(1)}, f32[12,512]{1,0:T(8,128)S(1)}, u32[]{:S(2)}, u32[]{:S(2)}) collective-permute-start(f32[12,512]{1,0:T(8,128)S(1)} %pad_maximum_fusion.12), channel_id=1, source_target_pairs={{0,8},{4,12},{8,16},{12,20},{16,24},{20,28},{24,0},{28,4},{1,9},{5... | collective-permute-start | bytes 73736 | tf_op jit(solution)/shard_map/ppermute | solution.py:95
  208.8 8.5 copy.204
  217.3 8.4 copy.205
  225.7 10.8 %fusion.3.weight_ref = bf16[4,2048,768]{2,1,0:T(8,128)(2,1)} fusion(bf16[4,2048,352]{2,1,0:T(8,128)(2,1)} %copy.205, bf16[4,2048,352]{2,1,0:T(8,128)(2,1)} %copy.204), kind=kLoop, calls=%fused_computation.6 | loop fusion | flops 50331648 | bytes 24117248 | tf_op jit(solution)/shard_map/concatenate | solution.py:541
  248.8 19.9 %fetch_rows.3 = bf16[4,1152,2048]{2,1,0:T(8,128)(2,1)} custom-call(s32[8,576,1]{2,1,0:T(8,128)} %sub.242.token_ref, bf16[8,512,2048]{2,1,0:T(8,128)(2,1)} %bitcast.328), custom_call_target="tpu_custom_call" | custom-call | flops 9663676416 | bytes 35651584 | tf_op jit(solution)/shard_map/fetch_rows/pallas_call | solution.py:243
  268.6 17.3 %fusion.116.grad_ref = f32[4,1152,352]{2,1,0:T(8,128)} fusion(bf16[4,1152,2048]{2,1,0:T(8,128)(2,1)} %fetch_rows.3, bf16[4,352,2048]{2,1,0:T(8,128)(2,1)} %param.34), kind=kOutput, calls=%fused_computation.354 | convolution fusion | flops 6643777536 | bytes 31129600 | tf_op jit(solution)/shard_map/erd,efd->erf/dot_general | solution.py:545
  285.9 29.4 %all-gather.7.cloned.1.call-done = bf16[4096,2048]{1,0:T(8,128)(2,1)} async-done(((bf16[128,2048]{1,0:T(8,128)(2,1)}), bf16[4096,2048]{1,0:T(8,128)(2,1)}) %all-gather.7.cloned.1.call-update) | async-done | bytes 16777232 | tf_op jit(solution)/shard_map/all_gather | solution.py:517
  315.4 19.2 %fetch_rows.2.rows_ref = bf16[4,1152,2048]{2,1,0:T(8,128)(2,1)} custom-call(s32[8,576,1]{2,1,0:T(8,128)} %sub.242.token_ref, bf16[8,512,2048]{2,1,0:T(8,128)(2,1)} %bitcast.329), custom_call_target="tpu_custom_call" | custom-call | flops 9663676416 | bytes 35651584 | tf_op jit(solution)/shard_map/fetch_rows/pallas_call | solution.py:243
  334.6 43.5 %expert_pass.1 = (bf16[4,1152,2048]{2,1,0:T(8,128)(2,1)}, bf16[4,1152,352]{2,1,0:T(8,128)(2,1)}, bf16[4,1152,352]{2,1,0:T(8,128)(2,1)}, bf16[4,1152,352]{2,1,0:T(8,128)(2,1)}, bf16[4,1152,352]{2,1,0:T(8,128)(2,1)}) custom-call(bf16[4,1152,2048]{2,1,0:T(8,128)(2,1)} %fetch_rows.2.rows_ref, f32[4,1152,352]{2,1,0:T(8,128)} %fusion.116.grad_ref, ...), custom_call_target="tpu_custom_call" | custom-call | flops 26575110144 | bytes 49283072 | tf_op jit(solution)/shard_map/expert_pass/pallas_call | solution.py:351
  378.1 11.3 %return_rows.4 = (bf16[4,128,1024]{2,1,0:T(8,128)(2,1)}, bf16[4,128,1024]{2,1,0:T(8,128)(2,1)}, bf16[4,128,1024]{2,1,0:T(8,128)(2,1)}, bf16[4,128,1024]{2,1,0:T(...) custom-call(s32[4]{0:T(128)} %add_subtract_fusion.order_ref, ...), custom_call_target="tpu_custom_call" | custom-call | flops 4831838208 | bytes 26214400 | tf_op jit(solution)/shard_map/return_rows/pallas_call | solution.py:292
  390.7 15.4 %fusion.118 = f32[4,2048,352]{1,2,0:T(8,128)} fusion(bf16[4,1152,2048]{2,1,0:T(8,128)(2,1)} %fetch_rows.2.rows_ref, bf16[4,1152,352]{2,1,0:T(8,128)(2,1)} %get-tuple-element.108), kind=kOutput, calls=%fused_computation.356 | convolution fusion | flops 6643777536 | bytes 33652736 | tf_op jit(solution)/shard_map/erd,erf->edf/dot_general | solution.py:570
  406.0 17.0 %fusion.rows_ref = bf16[4,1152,2048]{2,1,0:T(8,128)(2,1)} fusion(bf16[4,1152,352]{2,1,0:T(8,128)(2,1)} %get-tuple-element.76, bf16[4,352,2048]{2,1,0:T(8,128)(2,1)} %param.34, f32[4,1152]{1,0:T(4,128)S(1)} %mul.453), kind=kOutput, calls=%fused_computation.1 | convolution fusion | flops 6662651904 | bytes 27904000 | tf_op jit(solution)/shard_map/erf,efd->erd/dot_general | solution.py:562
  423.0 15.1 %fusion.119 = f32[4,2048,352]{1,2,0:T(8,128)} fusion(bf16[4,1152,2048]{2,1,0:T(8,128)(2,1)} %fetch_rows.2.rows_ref, bf16[4,1152,352]{2,1,0:T(8,128)(2,1)} %get-tuple-element.109), kind=kOutput, calls=%fused_computation.357 | convolution fusion | flops 6643777536 | bytes 33652736 | tf_op jit(solution)/shard_map/erd,erf->edf/dot_general | solution.py:573
  438.2 15.3 %fusion.117 = f32[4,352,2048]{2,1,0:T(8,128)} fusion(bf16[4,1152,352]{2,1,0:T(8,128)(2,1)} %get-tuple-element.107, bf16[4,1152,2048]{2,1,0:T(8,128)(2,1)} %fetch_rows.3), kind=kOutput, calls=%fused_computation.355 | convolution fusion | flops 6643777536 | bytes 33652736 | tf_op jit(solution)/shard_map/erf,erd->efd/dot_general | solution.py:567
  453.5 11.1 %return_rows.5 = (bf16[4,128,1024]{2,1,0:T(8,128)(2,1)}, bf16[4,128,1024]{2,1,0:T(8,128)(2,1)}, bf16[4,128,1024]{2,1,0:T(8,128)(2,1)}, bf16[4,128,1024]{2,1,0:T(...) custom-call(s32[4]{0:T(128)} %add_subtract_fusion.order_ref, ...), custom_call_target="tpu_custom_call" | custom-call | flops 4831838208 | bytes 26214400 | tf_op jit(solution)/shard_map/return_rows/pallas_call | solution.py:292
  464.6 8.5 fusion.15
  474.3 6.1 multiply_convert_fusion.3
  485.7 13.3 %return_rows.7 = (bf16[4,128,1024]{2,1,0:T(8,128)(2,1)}, bf16[4,128,1024]{2,1,0:T(8,128)(2,1)}, bf16[4,128,1024]{2,1,0:T(8,128)(2,1)}, bf16[4,128,1024]{2,1,0:T(...) custom-call(s32[4]{0:T(128)} %broadcast_add_fusion.1.order_ref, ...), custom_call_target="tpu_custom_call" | custom-call | flops 4831838208 | bytes 26214400 | tf_op jit(solution)/shard_map/return_rows/pallas_call | solution.py:292
  500.2 6.7 convolution_convert_fusion.7
  508.3 7.7 convolution_convert_fusion
  538.4 13.9 %return_rows.6 = (bf16[4,128,1024]{2,1,0:T(8,128)(2,1)}, bf16[4,128,1024]{2,1,0:T(8,128)(2,1)}, bf16[4,128,1024]{2,1,0:T(8,128)(2,1)}, bf16[4,128,1024]{2,1,0:T(...) custom-call(s32[4]{0:T(128)} %broadcast_add_fusion.1.order_ref, ...), custom_call_target="tpu_custom_call" | custom-call | flops 4831838208 | bytes 26214400 | tf_op jit(solution)/shard_map/return_rows/pallas_call | solution.py:292
  560.7 19.3 %collective-permute-done.77 = bf16[4,128,1024]{2,1,0:T(8,128)(2,1)} collective-permute-done((bf16[4,128,1024]{2,1,0:T(8,128)(2,1)}, bf16[4,128,1024]{2,1,0:T(8,128)(2,1)}, u32[]{:S(2)}, u32[]{:S(2)}) %collective-permute-start.77) | collective-permute-done | bytes 1048608 | tf_op jit(solution)/shard_map/ppermute | solution.py:152
  594.2 9.8 %collective-permute-done.79 = bf16[128,1024]{1,0:T(8,128)(2,1)S(1)} collective-permute-done((bf16[128,1024]{1,0:T(8,128)(2,1)S(1)}, bf16[128,1024]{1,0:T(8,128)(2,1)S(1)}, u32[]{:S(2)}, u32[]{:S(2)}) %collective-permute-start.79) | collective-permute-done | bytes 262176 | tf_op jit(solution)/shard_map/ppermute | solution.py:95
  605.4 6.5 collective-permute-start.85
  615.5 9.2 collective-permute-done.85
  631.9 11.2 %collective-permute-done.87 = bf16[128,2048]{1,0:T(8,128)(2,1)S(1)} collective-permute-done((bf16[128,2048]{1,0:T(8,128)(2,1)S(1)}, bf16[128,2048]{1,0:T(8,128)(2,1)S(1)}, u32[]{:S(2)}, u32[]{:S(2)}) %collective-permute-start.87) | collective-permute-done | bytes 524320 | tf_op jit(solution)/shard_map/ppermute | solution.py:89
  643.2 6.6 collective-permute-done.88
  656.4 23.6 %collective-permute-done.50 = bf16[4,128,1024]{2,1,0:T(8,128)(2,1)S(1)} collective-permute-done((bf16[4,128,1024]{2,1,0:T(8,128)(2,1)}, bf16[4,128,1024]{2,1,0:T(8,128)(2,1)S(1)}, u32[]{:S(2)}, u32[]{:S(2)}) %collective-permute-start.50) | collective-permute-done | bytes 1048608 | tf_op jit(solution)/shard_map/ppermute | solution.py:159
  721.3 10.7 %collective-permute-done.104 = bf16[8,64,576]{2,1,0:T(8,128)(2,1)S(1)} collective-permute-done((bf16[8,64,576]{2,1,0:T(8,128)(2,1)S(1)}, bf16[8,64,576]{2,1,0:T(8,128)(2,1)S(1)}, u32[]{:S(2)}, u32[]{:S(2)}) %collective-permute-start.104) | collective-permute-done | bytes 589856 | tf_op jit(solution)/shard_map/ppermute | solution.py:89
  743.4 32.7 %collective-permute-done.51 = bf16[4,128,1024]{2,1,0:T(8,128)(2,1)} collective-permute-done((bf16[4,128,1024]{2,1,0:T(8,128)(2,1)}, bf16[4,128,1024]{2,1,0:T(8,128)(2,1)}, u32[]{:S(2)}, u32[]{:S(2)}) %collective-permute-start.51) | collective-permute-done | bytes 1048608 | tf_op jit(solution)/shard_map/ppermute | solution.py:152
  777.6 8.0 collective-permute-start.52
  793.2 8.2 collective-permute-done.52
  804.8 11.1 %collective-permute-done.53 = bf16[128,1024]{1,0:T(8,128)(2,1)S(1)} collective-permute-done((bf16[128,1024]{1,0:T(8,128)(2,1)S(1)}, bf16[128,1024]{1,0:T(8,128)(2,1)S(1)}, u32[]{:S(2)}, u32[]{:S(2)}) %collective-permute-start.53) | collective-permute-done | bytes 262176 | tf_op jit(solution)/shard_map/ppermute | solution.py:95
  819.7 13.6 %collective-permute-done.58 = bf16[128,1024]{1,0:T(8,128)(2,1)S(1)} collective-permute-done((bf16[128,1024]{1,0:T(8,128)(2,1)S(1)}, bf16[128,1024]{1,0:T(8,128)(2,1)S(1)}, u32[]{:S(2)}, u32[]{:S(2)}) %collective-permute-start.58) | collective-permute-done | bytes 262176 | tf_op jit(solution)/shard_map/ppermute | solution.py:95
  833.3 18.3 %collective-permute-done.59 = bf16[128,1024]{1,0:T(8,128)(2,1)S(1)} collective-permute-done((bf16[128,1024]{1,0:T(8,128)(2,1)S(1)}, bf16[128,1024]{1,0:T(8,128)(2,1)S(1)}, u32[]{:S(2)}, u32[]{:S(2)}) %collective-permute-start.59) | collective-permute-done | bytes 262176 | tf_op jit(solution)/shard_map/ppermute | solution.py:95
  864.7 5.9 collective-permute-done.61
  873.9 8.0 collective-permute-done.62
  882.6 10.4 %collective-permute-done.90 = bf16[128,2048]{1,0:T(8,128)(2,1)S(1)} collective-permute-done((bf16[128,2048]{1,0:T(8,128)(2,1)}, bf16[128,2048]{1,0:T(8,128)(2,1)S(1)}, u32[]{:S(2)}, u32[]{:S(2)}) %collective-permute-start.90) | collective-permute-done | bytes 524320 | tf_op jit(solution)/shard_map/ppermute | solution.py:89
  893.0 9.6 collective-permute-done.91
  929.9 8.7 collective-permute-done.94
  946.9 9.0 collective-permute-start.100
  (597 shorter events, 332.2 us)
Async XLA Ops:
  7.2 177.1 %all-gather.5.cloned.1.call-start = ((), (), s32[]{:S(2)}) async-start(), calls=%async_computation.4 | async-start | bytes 17301504 | tf_op jit(solution)/shard_map/all_gather | solution.py:450
  22.1 293.2 %all-gather.7.cloned.1.call-start = ((), (), s32[]{:S(2)}) async-start(), calls=%async_computation.5 | async-start | bytes 17301504 | tf_op jit(solution)/shard_map/all_gather | solution.py:517
  22.2 83.4 %collective-permute-start.17 = (bf16[256,768]{1,0:T(8,128)(2,1)}, bf16[256,768]{1,0:T(8,128)(2,1)}, u32[]{:S(2)}, u32[]{:S(2)}) collective-permute-start(bf16[256,768]{1,0:T(8,128)(2,1)} %param.23), channel_id=1, source_target_pairs={{0,8},{4,12},{8,16},{12,20},{16,24},{20,28},{24,0},{28,4},{1,9},{5... | collective-permute-start | bytes 1179656 | tf_op jit(solution)/shard_map/ppermute | solution.py:95
  24.2 81.5 %collective-permute-start.18 = (bf16[256,768]{1,0:T(8,128)(2,1)}, bf16[256,768]{1,0:T(8,128)(2,1)}, u32[]{:S(2)}, u32[]{:S(2)}) collective-permute-start(bf16[256,768]{1,0:T(8,128)(2,1)} %param.23), channel_id=1, source_target_pairs={{0,16},{4,20},{8,24},{12,28},{16,0},{20,4},{24,8},{28,12},{1,17},{... | collective-permute-start | bytes 1179656 | tf_op jit(solution)/shard_map/ppermute | solution.py:95
  28.9 33.6 %collective-permute-start.8 = (bf16[8,64,579]{2,1,0:T(8,128)(2,1)S(1)}, bf16[8,64,579]{2,1,0:T(8,128)(2,1)S(1)}, u32[]{:S(2)}, u32[]{:S(2)}) collective-permute-start(bf16[8,64,579]{2,1,0:T(8,128)(2,1)S(1)} %bitcast_dynamic-update-slice_fusion.40), channel_id=1, source_target_pairs={{0,2},{1,3},{2,0},{3,1},{4,6},{5,7},{6,4},{7,5},{8,10},{9,11},{10,... | collective-permute-start | bytes 1778696 | tf_op jit(solution)/shard_map/ppermute | solution.py:89
  30.9 31.8 %collective-permute-start.9 = (bf16[8,64,579]{2,1,0:T(8,128)(2,1)S(1)}, bf16[8,64,579]{2,1,0:T(8,128)(2,1)S(1)}, u32[]{:S(2)}, u32[]{:S(2)}) collective-permute-start(bf16[8,64,579]{2,1,0:T(8,128)(2,1)S(1)} %bitcast_dynamic-update-slice_fusion.40), channel_id=1, source_target_pairs={{0,3},{1,0},{2,1},{3,2},{4,7},{5,4},{6,5},{7,6},{8,11},{9,8},{10,9... | collective-permute-start | bytes 1778696 | tf_op jit(solution)/shard_map/ppermute | solution.py:89
  49.7 56.4 %collective-permute-start.19 = (bf16[256,768]{1,0:T(8,128)(2,1)}, bf16[256,768]{1,0:T(8,128)(2,1)}, u32[]{:S(2)}, u32[]{:S(2)}) collective-permute-start(bf16[256,768]{1,0:T(8,128)(2,1)} %param.23), channel_id=1, source_target_pairs={{0,24},{4,28},{8,0},{12,4},{16,8},{20,12},{24,16},{28,20},{1,25},{... | collective-permute-start | bytes 1179656 | tf_op jit(solution)/shard_map/ppermute | solution.py:95
  62.5 54.2 %collective-permute-start.20 = (bf16[256,768]{1,0:T(8,128)(2,1)}, bf16[256,768]{1,0:T(8,128)(2,1)}, u32[]{:S(2)}, u32[]{:S(2)}) collective-permute-start(bf16[256,768]{1,0:T(8,128)(2,1)} %param.23), channel_id=1, source_target_pairs={{0,4},{4,0},{8,12},{12,8},{16,20},{20,16},{24,28},{28,24},{1,5},{5... | collective-permute-start | bytes 1179656 | tf_op jit(solution)/shard_map/ppermute | solution.py:99
  106.5 34.7 %collective-permute-start.24 = (bf16[512,256]{0,1:T(8,128)(2,1)}, bf16[512,256]{0,1:T(8,128)(2,1)}, u32[]{:S(2)}, u32[]{:S(2)}) collective-permute-start(bf16[512,256]{0,1:T(8,128)(2,1)} %copy.191), channel_id=1, source_target_pairs={{0,8},{4,12},{8,16},{12,20},{16,24},{20,28},{24,0},{28,4},{1,9},{5... | collective-permute-start | bytes 786440 | tf_op jit(solution)/shard_map/ppermute | solution.py:95
  116.7 29.7 %collective-permute-start.25 = (bf16[512,256]{0,1:T(8,128)(2,1)}, bf16[512,256]{0,1:T(8,128)(2,1)}, u32[]{:S(2)}, u32[]{:S(2)}) collective-permute-start(bf16[512,256]{0,1:T(8,128)(2,1)} %copy.191), channel_id=1, source_target_pairs={{0,16},{4,20},{8,24},{12,28},{16,0},{20,4},{24,8},{28,12},{1,17},{... | collective-permute-start | bytes 786440 | tf_op jit(solution)/shard_map/ppermute | solution.py:95
  187.7 276.9 %all-gather.9.cloned.1.call-start = ((), (), s32[]{:S(2)}) async-start(), calls=%async_computation.6 | async-start | bytes 6488064 | tf_op jit(solution)/shard_map/all_gather | solution.py:520
  188.7 285.6 %all-gather.11.cloned.1.call-start = ((), (), s32[]{:S(2)}) async-start(), calls=%async_computation.7 | async-start | bytes 3244032 | tf_op jit(solution)/shard_map/all_gather | solution.py:523
  188.8 48.3 %collective-permute-start.34 = (f32[12,512]{1,0:T(8,128)S(1)}, f32[12,512]{1,0:T(8,128)S(1)}, u32[]{:S(2)}, u32[]{:S(2)}) collective-permute-start(f32[12,512]{1,0:T(8,128)S(1)} %pad_maximum_fusion.12), channel_id=1, source_target_pairs={{0,8},{4,12},{8,16},{12,20},{16,24},{20,28},{24,0},{28,4},{1,9},{5... | collective-permute-start | bytes 73736 | tf_op jit(solution)/shard_map/ppermute | solution.py:95
  205.1 32.4 %collective-permute-start.35 = (f32[12,512]{1,0:T(8,128)S(1)}, f32[12,512]{1,0:T(8,128)S(1)}, u32[]{:S(2)}, u32[]{:S(2)}) collective-permute-start(f32[12,512]{1,0:T(8,128)S(1)} %pad_maximum_fusion.12), channel_id=1, source_target_pairs={{0,16},{4,20},{8,24},{12,28},{16,0},{20,4},{24,8},{28,12},{1,17},{... | collective-permute-start | bytes 73736 | tf_op jit(solution)/shard_map/ppermute | solution.py:95
  205.1 32.5 %collective-permute-start.36 = (f32[12,512]{1,0:T(8,128)S(1)}, f32[12,512]{1,0:T(8,128)S(1)}, u32[]{:S(2)}, u32[]{:S(2)}) collective-permute-start(f32[12,512]{1,0:T(8,128)S(1)} %pad_maximum_fusion.12), channel_id=1, source_target_pairs={{0,24},{4,28},{8,0},{12,4},{16,8},{20,12},{24,16},{28,20},{1,25},{... | collective-permute-start | bytes 73736 | tf_op jit(solution)/shard_map/ppermute | solution.py:95
  207.6 30.8 %collective-permute-start.37 = (f32[12,512]{1,0:T(8,128)S(1)}, f32[12,512]{1,0:T(8,128)S(1)}, u32[]{:S(2)}, u32[]{:S(2)}) collective-permute-start(f32[12,512]{1,0:T(8,128)S(1)} %pad_maximum_fusion.12), channel_id=1, source_target_pairs={{0,4},{4,0},{8,12},{12,8},{16,20},{20,16},{24,28},{28,24},{1,5},{5... | collective-permute-start | bytes 73736 | tf_op jit(solution)/shard_map/ppermute | solution.py:99
  207.6 734.3 %reduce-scatter.7.cloned.1.call-start = ((), (), s32[]{:S(2)}) async-start(), calls=%async_computation.9 | async-start | bytes 3244032 | tf_op jit(solution)/shard_map/reduce_scatter | solution.py:685
  389.4 83.7 %collective-permute-start.67 = (bf16[4,128,1024]{2,1,0:T(8,128)(2,1)}, bf16[4,128,1024]{2,1,0:T(8,128)(2,1)S(1)}, u32[]{:S(2)}, u32[]{:S(2)}) collective-permute-start(bf16[4,128,1024]{2,1,0:T(8,128)(2,1)} %get-tuple-element.75), channel_id=1, source_target_pairs={{0,4},{4,0},{8,12},{12,8},{16,20},{20,16},{24,28},{28,24},{1,5},{5... | collective-permute-start | bytes 3145736 | tf_op jit(solution)/shard_map/ppermute | solution.py:99
  389.7 83.7 %collective-permute-start.68 = (bf16[4,128,1024]{2,1,0:T(8,128)(2,1)}, bf16[4,128,1024]{2,1,0:T(8,128)(2,1)}, u32[]{:S(2)}, u32[]{:S(2)}) collective-permute-start(bf16[4,128,1024]{2,1,0:T(8,128)(2,1)} %get-tuple-element.93), channel_id=1, source_target_pairs={{0,4},{4,0},{8,12},{12,8},{16,20},{20,16},{24,28},{28,24},{1,5},{5... | collective-permute-start | bytes 3145736 | tf_op jit(solution)/shard_map/ppermute | solution.py:99
  389.9 83.7 %collective-permute-start.69 = (bf16[4,128,1024]{2,1,0:T(8,128)(2,1)}, bf16[4,128,1024]{2,1,0:T(8,128)(2,1)}, u32[]{:S(2)}, u32[]{:S(2)}) collective-permute-start(bf16[4,128,1024]{2,1,0:T(8,128)(2,1)} %get-tuple-element.94), channel_id=1, source_target_pairs={{0,4},{4,0},{8,12},{12,8},{16,20},{20,16},{24,28},{28,24},{1,5},{5... | collective-permute-start | bytes 3145736 | tf_op jit(solution)/shard_map/ppermute | solution.py:99
  390.2 83.7 %collective-permute-start.70 = (bf16[4,128,1024]{2,1,0:T(8,128)(2,1)}, bf16[4,128,1024]{2,1,0:T(8,128)(2,1)}, u32[]{:S(2)}, u32[]{:S(2)}) collective-permute-start(bf16[4,128,1024]{2,1,0:T(8,128)(2,1)} %get-tuple-element.95), channel_id=1, source_target_pairs={{0,4},{4,0},{8,12},{12,8},{16,20},{20,16},{24,28},{28,24},{1,5},{5... | collective-permute-start | bytes 3145736 | tf_op jit(solution)/shard_map/ppermute | solution.py:99
  390.4 94.2 %collective-permute-start.71 = (bf16[4,128,1024]{2,1,0:T(8,128)(2,1)}, bf16[4,128,1024]{2,1,0:T(8,128)(2,1)}, u32[]{:S(2)}, u32[]{:S(2)}) collective-permute-start(bf16[4,128,1024]{2,1,0:T(8,128)(2,1)} %get-tuple-element.96), channel_id=1, source_target_pairs={{0,4},{4,0},{8,12},{12,8},{16,20},{20,16},{24,28},{28,24},{1,5},{5... | collective-permute-start | bytes 3145736 | tf_op jit(solution)/shard_map/ppermute | solution.py:99
  484.6 459.2 %reduce-scatter.9.cloned.1.call-start = ((), (), s32[]{:S(2)}) async-start(), calls=%async_computation.10 | async-start | bytes 2359296 | tf_op jit(solution)/shard_map/reduce_scatter | solution.py:688
  485.0 31.0 %collective-permute-start.43 = (bf16[4,128,1024]{2,1,0:T(8,128)(2,1)}, bf16[4,128,1024]{2,1,0:T(8,128)(2,1)}, u32[]{:S(2)}, u32[]{:S(2)}) collective-permute-start(bf16[4,128,1024]{2,1,0:T(8,128)(2,1)} %get-tuple-element.79), channel_id=1, source_target_pairs={{0,4},{4,0},{8,12},{12,8},{16,20},{20,16},{24,28},{28,24},{1,5},{5... | collective-permute-start | bytes 3145736 | tf_op jit(solution)/shard_map/ppermute | solution.py:99
  485.2 30.9 %collective-permute-start.44 = (bf16[4,128,1024]{2,1,0:T(8,128)(2,1)}, bf16[4,128,1024]{2,1,0:T(8,128)(2,1)}, u32[]{:S(2)}, u32[]{:S(2)}) collective-permute-start(bf16[4,128,1024]{2,1,0:T(8,128)(2,1)} %get-tuple-element.80), channel_id=1, source_target_pairs={{0,4},{4,0},{8,12},{12,8},{16,20},{20,16},{24,28},{28,24},{1,5},{5... | collective-permute-start | bytes 3145736 | tf_op jit(solution)/shard_map/ppermute | solution.py:99
  485.5 31.0 %collective-permute-start.45 = (bf16[4,128,1024]{2,1,0:T(8,128)(2,1)}, bf16[4,128,1024]{2,1,0:T(8,128)(2,1)}, u32[]{:S(2)}, u32[]{:S(2)}) collective-permute-start(bf16[4,128,1024]{2,1,0:T(8,128)(2,1)} %get-tuple-element.81), channel_id=1, source_target_pairs={{0,4},{4,0},{8,12},{12,8},{16,20},{20,16},{24,28},{28,24},{1,5},{5... | collective-permute-start | bytes 3145736 | tf_op jit(solution)/shard_map/ppermute | solution.py:99
  536.7 43.4 %collective-permute-start.77 = (bf16[4,128,1024]{2,1,0:T(8,128)(2,1)}, bf16[4,128,1024]{2,1,0:T(8,128)(2,1)}, u32[]{:S(2)}, u32[]{:S(2)}) collective-permute-start(bf16[4,128,1024]{2,1,0:T(8,128)(2,1)} %add_convert_fusion.3), channel_id=1, source_target_pairs={{0,2},{1,3},{2,0},{3,1},{4,6},{5,7},{6,4},{7,5},{8,10},{9,11},{10,... | collective-permute-start | bytes 3145736 | tf_op jit(solution)/shard_map/ppermute | solution.py:152
  537.3 48.2 %collective-permute-start.83 = (bf16[4,128,1024]{2,1,0:T(8,128)(2,1)}, bf16[4,128,1024]{2,1,0:T(8,128)(2,1)}, u32[]{:S(2)}, u32[]{:S(2)}) collective-permute-start(bf16[4,128,1024]{2,1,0:T(8,128)(2,1)} %add_convert_fusion.1), channel_id=1, source_target_pairs={{0,1},{1,0},{2,3},{3,2},{4,5},{5,4},{6,7},{7,6},{8,9},{9,8},{10,11... | collective-permute-start | bytes 3145736 | tf_op jit(solution)/shard_map/ppermute | solution.py:159
  587.8 37.1 %collective-permute-start.64 = (bf16[128,2048]{1,0:T(8,128)(2,1)S(1)}, bf16[128,2048]{1,0:T(8,128)(2,1)S(1)}, u32[]{:S(2)}, u32[]{:S(2)}) collective-permute-start(bf16[128,2048]{1,0:T(8,128)(2,1)S(1)} %get-tuple-element.224), channel_id=1, source_target_pairs={{0,1},{1,2},{2,3},{3,0},{4,5},{5,6},{6,7},{7,4},{8,9},{9,10},{10,1... | collective-permute-start | bytes 1572872 | tf_op jit(solution)/shard_map/ppermute | solution.py:89
  592.7 32.2 %collective-permute-start.65 = (bf16[128,2048]{1,0:T(8,128)(2,1)S(1)}, bf16[128,2048]{1,0:T(8,128)(2,1)S(1)}, u32[]{:S(2)}, u32[]{:S(2)}) collective-permute-start(bf16[128,2048]{1,0:T(8,128)(2,1)S(1)} %get-tuple-element.226), channel_id=1, source_target_pairs={{0,2},{1,3},{2,0},{3,1},{4,6},{5,7},{6,4},{7,5},{8,10},{9,11},{10,... | collective-permute-start | bytes 1572872 | tf_op jit(solution)/shard_map/ppermute | solution.py:89
  652.6 293.0 %reduce-scatter.5.cloned.1.call-start = ((), (), s32[]{:S(2)}) async-start(), calls=%async_computation.8 | async-start | bytes 6488064 | tf_op jit(solution)/shard_map/reduce_scatter | solution.py:680
  653.4 312.6 %reduce-scatter.11.cloned.1.call-start = ((), (), s32[]{:S(2)}) async-start(), calls=%async_computation.11 | async-start | bytes 5455872 | tf_op jit(solution)/shard_map/reduce_scatter | solution.py:701
  655.5 86.3 %collective-permute-start.49 = (bf16[4,128,1024]{2,1,0:T(8,128)(2,1)}, bf16[4,128,1024]{2,1,0:T(8,128)(2,1)}, u32[]{:S(2)}, u32[]{:S(2)}) collective-permute-start(bf16[4,128,1024]{2,1,0:T(8,128)(2,1)} %get-tuple-element.86), channel_id=1, source_target_pairs={{0,1},{1,0},{2,3},{3,2},{4,5},{5,4},{6,7},{7,6},{8,9},{9,8},{10,11... | collective-permute-start | bytes 3145736 | tf_op jit(solution)/shard_map/ppermute | solution.py:159
  655.7 79.1 %collective-permute-start.56 = (bf16[4,128,1024]{2,1,0:T(8,128)(2,1)}, bf16[4,128,1024]{2,1,0:T(8,128)(2,1)}, u32[]{:S(2)}, u32[]{:S(2)}) collective-permute-start(bf16[4,128,1024]{2,1,0:T(8,128)(2,1)} %get-tuple-element.92), channel_id=1, source_target_pairs={{0,2},{1,3},{2,0},{3,1},{4,6},{5,7},{6,4},{7,5},{8,10},{9,11},{10,... | collective-permute-start | bytes 3145736 | tf_op jit(solution)/shard_map/ppermute | solution.py:152
  703.9 28.1 %collective-permute-start.104 = (bf16[8,64,576]{2,1,0:T(8,128)(2,1)S(1)}, bf16[8,64,576]{2,1,0:T(8,128)(2,1)S(1)}, u32[]{:S(2)}, u32[]{:S(2)}) collective-permute-start(bf16[8,64,576]{2,1,0:T(8,128)(2,1)S(1)} %get-tuple-element.219), channel_id=1, source_target_pairs={{0,2},{1,3},{2,0},{3,1},{4,6},{5,7},{6,4},{7,5},{8,10},{9,11},{10,... | collective-permute-start | bytes 1769480 | tf_op jit(solution)/shard_map/ppermute | solution.py:89
  704.4 27.6 %collective-permute-start.105 = (bf16[8,64,576]{2,1,0:T(8,128)(2,1)S(1)}, bf16[8,64,576]{2,1,0:T(8,128)(2,1)S(1)}, u32[]{:S(2)}, u32[]{:S(2)}) collective-permute-start(bf16[8,64,576]{2,1,0:T(8,128)(2,1)S(1)} %get-tuple-element.218), channel_id=1, source_target_pairs={{0,3},{1,0},{2,1},{3,2},{4,7},{5,4},{6,5},{7,6},{8,11},{9,8},{10,9... | collective-permute-start | bytes 1769480 | tf_op jit(solution)/shard_map/ppermute | solution.py:89
  720.7 68.4 %collective-permute-start.55 = (bf16[4,128,1024]{2,1,0:T(8,128)(2,1)}, bf16[4,128,1024]{2,1,0:T(8,128)(2,1)}, u32[]{:S(2)}, u32[]{:S(2)}) collective-permute-start(bf16[4,128,1024]{2,1,0:T(8,128)(2,1)} %get-tuple-element.90), channel_id=1, source_target_pairs={{0,2},{1,3},{2,0},{3,1},{4,6},{5,7},{6,4},{7,5},{8,10},{9,11},{10,... | collective-permute-start | bytes 3145736 | tf_op jit(solution)/shard_map/ppermute | solution.py:152
  732.0 44.1 %collective-permute-start.51 = (bf16[4,128,1024]{2,1,0:T(8,128)(2,1)}, bf16[4,128,1024]{2,1,0:T(8,128)(2,1)}, u32[]{:S(2)}, u32[]{:S(2)}) collective-permute-start(bf16[4,128,1024]{2,1,0:T(8,128)(2,1)} %add_convert_fusion.7), channel_id=1, source_target_pairs={{0,2},{1,3},{2,0},{3,1},{4,6},{5,7},{6,4},{7,5},{8,10},{9,11},{10,... | collective-permute-start | bytes 3145736 | tf_op jit(solution)/shard_map/ppermute | solution.py:152
  736.9 53.9 %collective-permute-start.57 = (bf16[4,128,1024]{2,1,0:T(8,128)(2,1)S(1)}, bf16[4,128,1024]{2,1,0:T(8,128)(2,1)S(1)}, u32[]{:S(2)}, u32[]{:S(2)}) collective-permute-start(bf16[4,128,1024]{2,1,0:T(8,128)(2,1)S(1)} %add_convert_fusion.5), channel_id=1, source_target_pairs={{0,1},{1,0},{2,3},{3,2},{4,5},{5,4},{6,7},{7,6},{8,9},{9,8},{10,11... | collective-permute-start | bytes 3145736 | tf_op jit(solution)/shard_map/ppermute | solution.py:159
  785.6 30.3 %collective-permute-start.53 = (bf16[128,1024]{1,0:T(8,128)(2,1)S(1)}, bf16[128,1024]{1,0:T(8,128)(2,1)S(1)}, u32[]{:S(2)}, u32[]{:S(2)}) collective-permute-start(bf16[128,1024]{1,0:T(8,128)(2,1)S(1)} %get-tuple-element.237), channel_id=1, source_target_pairs={{0,16},{4,20},{8,24},{12,28},{16,0},{20,4},{24,8},{28,12},{1,17},{... | collective-permute-start | bytes 786440 | tf_op jit(solution)/shard_map/ppermute | solution.py:95
  789.1 29.5 %collective-permute-start.54 = (bf16[128,1024]{1,0:T(8,128)(2,1)S(1)}, bf16[128,1024]{1,0:T(8,128)(2,1)S(1)}, u32[]{:S(2)}, u32[]{:S(2)}) collective-permute-start(bf16[128,1024]{1,0:T(8,128)(2,1)S(1)} %get-tuple-element.236), channel_id=1, source_target_pairs={{0,24},{4,28},{8,0},{12,4},{16,8},{20,12},{24,16},{28,20},{1,25},{... | collective-permute-start | bytes 786440 | tf_op jit(solution)/shard_map/ppermute | solution.py:95
  791.1 42.2 %collective-permute-start.58 = (bf16[128,1024]{1,0:T(8,128)(2,1)S(1)}, bf16[128,1024]{1,0:T(8,128)(2,1)S(1)}, u32[]{:S(2)}, u32[]{:S(2)}) collective-permute-start(bf16[128,1024]{1,0:T(8,128)(2,1)S(1)} %get-tuple-element.238), channel_id=1, source_target_pairs={{0,8},{4,12},{8,16},{12,20},{16,24},{20,28},{24,0},{28,4},{1,9},{5... | collective-permute-start | bytes 786440 | tf_op jit(solution)/shard_map/ppermute | solution.py:95
  793.2 58.5 %collective-permute-start.59 = (bf16[128,1024]{1,0:T(8,128)(2,1)S(1)}, bf16[128,1024]{1,0:T(8,128)(2,1)S(1)}, u32[]{:S(2)}, u32[]{:S(2)}) collective-permute-start(bf16[128,1024]{1,0:T(8,128)(2,1)S(1)} %get-tuple-element.240), channel_id=1, source_target_pairs={{0,16},{4,20},{8,24},{12,28},{16,0},{20,4},{24,8},{28,12},{1,17},{... | collective-permute-start | bytes 786440 | tf_op jit(solution)/shard_map/ppermute | solution.py:95
  801.3 50.3 %collective-permute-start.60 = (bf16[128,1024]{1,0:T(8,128)(2,1)S(1)}, bf16[128,1024]{1,0:T(8,128)(2,1)S(1)}, u32[]{:S(2)}, u32[]{:S(2)}) collective-permute-start(bf16[128,1024]{1,0:T(8,128)(2,1)S(1)} %get-tuple-element.239), channel_id=1, source_target_pairs={{0,24},{4,28},{8,0},{12,4},{16,8},{20,12},{24,16},{28,20},{1,25},{... | collective-permute-start | bytes 786440 | tf_op jit(solution)/shard_map/ppermute | solution.py:95
  859.8 58.4 %collective-permute-start.63 = (bf16[128,2048]{1,0:T(8,128)(2,1)}, bf16[128,2048]{1,0:T(8,128)(2,1)}, u32[]{:S(2)}, u32[]{:S(2)}) collective-permute-start(bf16[128,2048]{1,0:T(8,128)(2,1)} %get-tuple-element.209), channel_id=1, source_target_pairs={{0,3},{1,0},{2,1},{3,2},{4,7},{5,4},{6,5},{7,6},{8,11},{9,8},{10,9... | collective-permute-start | bytes 1572872 | tf_op jit(solution)/shard_map/ppermute | solution.py:89
  863.5 29.5 %collective-permute-start.90 = (bf16[128,2048]{1,0:T(8,128)(2,1)}, bf16[128,2048]{1,0:T(8,128)(2,1)S(1)}, u32[]{:S(2)}, u32[]{:S(2)}) collective-permute-start(bf16[128,2048]{1,0:T(8,128)(2,1)} %get-tuple-element.221), channel_id=1, source_target_pairs={{0,1},{1,2},{2,3},{3,0},{4,5},{5,6},{6,7},{7,4},{8,9},{9,10},{10,1... | collective-permute-start | bytes 1572872 | tf_op jit(solution)/shard_map/ppermute | solution.py:89
  864.4 38.2 %collective-permute-start.91 = (bf16[128,2048]{1,0:T(8,128)(2,1)}, bf16[128,2048]{1,0:T(8,128)(2,1)S(1)}, u32[]{:S(2)}, u32[]{:S(2)}) collective-permute-start(bf16[128,2048]{1,0:T(8,128)(2,1)} %get-tuple-element.223), channel_id=1, source_target_pairs={{0,2},{1,3},{2,0},{3,1},{4,6},{5,7},{6,4},{7,5},{8,10},{9,11},{10,... | collective-permute-start | bytes 1572872 | tf_op jit(solution)/shard_map/ppermute | solution.py:89
  870.6 32.8 %collective-permute-start.92 = (bf16[128,2048]{1,0:T(8,128)(2,1)}, bf16[128,2048]{1,0:T(8,128)(2,1)}, u32[]{:S(2)}, u32[]{:S(2)}) collective-permute-start(bf16[128,2048]{1,0:T(8,128)(2,1)} %get-tuple-element.222), channel_id=1, source_target_pairs={{0,3},{1,0},{2,1},{3,2},{4,7},{5,4},{6,5},{7,6},{8,11},{9,8},{10,9... | collective-permute-start | bytes 1572872 | tf_op jit(solution)/shard_map/ppermute | solution.py:89
  (154 other events, 1883.1 us)
Sparse Core Ops, SparseCore 0:
  22.3 160.0 all-gather.4
  187.8 127.5 all-gather.6
  317.5 59.0 all-gather.8
  378.0 35.2 all-gather.10
  484.7 37.1 reduce-scatter.6
  652.7 43.5 reduce-scatter.8
  698.7 63.4 reduce-scatter.4
  764.5 81.5 reduce-scatter.10

commit v2 on v1

--- a/solution.py
+++ b/solution.py
@@ -580,9 +580,8 @@
     )
     shared_gate_act, shared_up_act = gate_lift_act[:, :hidden_width], gate_lift_act[:, hidden_width:]
     shared_hidden = (jax.nn.silu(shared_gate_act) * shared_up_act).astype(jnp.bfloat16)
-    shared_out = jnp.dot(shared_hidden, lower_full, preferred_element_type=jnp.float32).astype(
-        jnp.bfloat16
-    )
+    shared_out = jnp.dot(shared_hidden, lower_full, preferred_element_type=jnp.float32)
+    shared_out = shared_out.astype(jnp.bfloat16)
     out_cut, out_other = cut_back(expert_out, shared_out)
     block_out = scatter_all(out_cut)
     output_share = (middle + block_out).astype(jnp.bfloat16)
@@ -667,16 +666,6 @@
     ]
     grad_normed_one = dot_last(grad_queries, query_full)
     grad_normed_one = grad_normed_one + dot_last(grad_compressed, latent_full)
-    grad_normed_one = grad_normed_one.astype(jnp.bfloat16)
-    grad_latent_part = total([after(latent_parts[0], grad_normed_one)] + latent_parts[1:])
-    grad_normed_one = scatter_tensor(grad_normed_one)
-    hat_one_share = quarter(hat_one)
-    grad_gain_one = jnp.sum(grad_normed_one * hat_one_share, axis=0)
-    grad_tokens = grad_middle + norm_back(
-        grad_normed_one * attention_norm_scale, hat_one_share, quarter(inv_one)
-    )
-    grad_tokens = gather_tensor(grad_tokens.astype(jnp.bfloat16)).astype(jnp.float32)
-
     grad_gate_lift_share = lax.psum_scatter(
         grad_gate_lift_full, DP, scatter_dimension=0, tiled=True
     ).astype(jnp.float32)
@@ -688,6 +677,16 @@
     grad_out_weight = lax.psum_scatter(
         grad_output_full.astype(jnp.bfloat16), DP, scatter_dimension=1, tiled=True
     ).astype(jnp.float32)
+    grad_normed_one = grad_normed_one.astype(jnp.bfloat16)
+    grad_latent_part = total([after(latent_parts[0], grad_query_full)] + latent_parts[1:])
+    grad_normed_one = scatter_tensor(grad_normed_one)
+    hat_one_share = quarter(hat_one)
+    grad_gain_one = jnp.sum(grad_normed_one * hat_one_share, axis=0)
+    grad_tokens = grad_middle + norm_back(
+        grad_normed_one * attention_norm_scale, hat_one_share, quarter(inv_one)
+    )
+    grad_tokens = gather_tensor(grad_tokens.astype(jnp.bfloat16)).astype(jnp.float32)
+
     query_width, expand_width = 4 * q_weight.shape[1], kvb_weight.shape[1]
     packed_rows = grad_expand_full.shape[0]
     packed_grad = jnp.concatenate(

time: 991 us -> 975 us (0.984)
  waiting for transfers between devices: 356 us -> 328 us
    ppermute x6, waiting for transfers between devices: 61.1 us -> 39.9 us  [shift_outer(): return lax.ppermute(value, TP, pairs)]
    unnamed x185 -> x201, local copies, waits for them, and re-layouts: 32 us -> 35.5 us
  transfers between devices with their start and end apart: 114 -> 114, of which waited for: 46 -> 47; matrix products, arithmetic and copies ran while one was open for 31% -> 31% of each run, Pallas kernels for 14% -> 14%
where the time goes in v2:
time: 975 us; the launch traced here: 964 us
  waiting for transfers between devices  328 us (34%)
  starting transfers between devices  162 us (17%)
  matrix products  151 us (15%)
  Pallas kernels  132 us (14%)
  local copies, waits for them, and re-layouts  94 us (10%)
  other arithmetic  80.7 us (8%)
  between operations  16.4 us (2%)
    ppermute x27, waiting for transfers between devices, shift_tensor(): lax.ppermute(value, TP, [(i, (i + step) % size) for i in range(size)])  133 us
    ppermute x30, starting transfers between devices, shift_chips(): return lax.ppermute(value, DP, pairs)  100 us
    ppermute x30, waiting for transfers between devices, shift_chips(): return lax.ppermute(value, DP, pairs)  97.1 us
    pallas_call x4, Pallas kernels, return_rows(): pl.pallas_call(functools.partial(return_kernel, extra is not None), grid_...  49.4 us
    pallas_call x1, Pallas kernels, expert_pass(): pl.pallas_call(expert_kernel, grid=(experts, 2), in_specs=[row_spec, hidd...  43.5 us
    ppermute x6, waiting for transfers between devices, shift_outer(): return lax.ppermute(value, TP, pairs)  39.9 us
    pallas_call x2, Pallas kernels, fetch_rows(): pl.pallas_call(fetch_kernel, grid=(ranks,), in_specs=[pl.BlockSpec((None,...  39.1 us
    ppermute x27, starting transfers between devices, shift_tensor(): lax.ppermute(value, TP, [(i, (i + step) % size) for i in range(size)])  36.9 us
  transfers between devices with their start and end apart: 114, of which 47 were waited for; matrix products, arithmetic and copies ran while one was open for 31% of the time, Pallas kernels for 14%

profile of v2, /device:TPU:0, one launch (start us, length us, event | category | flops | bytes accessed | tf_op | source)
XLA Modules:
  0.0 963.6 jit_solution(12067513509560745245)
XLA Ops:
  32.8 16.9 %collective-permute-done.7 = bf16[8,64,579]{2,1,0:T(8,128)(2,1)S(1)} collective-permute-done((bf16[8,64,579]{2,1,0:T(8,128)(2,1)S(1)}, bf16[8,64,579]{2,1,0:T(8,128)(2,1)S(1)}, u32[]{:S(2)}, u32[]{:S(2)}) %collective-permute-start.7) | collective-permute-done | bytes 592928 | tf_op jit(solution)/shard_map/ppermute | solution.py:89
  50.7 11.8 %collective-permute-done.8 = bf16[8,64,579]{2,1,0:T(8,128)(2,1)S(1)} collective-permute-done((bf16[8,64,579]{2,1,0:T(8,128)(2,1)S(1)}, bf16[8,64,579]{2,1,0:T(8,128)(2,1)S(1)}, u32[]{:S(2)}, u32[]{:S(2)}) %collective-permute-start.8) | collective-permute-done | bytes 592928 | tf_op jit(solution)/shard_map/ppermute | solution.py:89
  76.0 10.9 %collective-permute-done.11 = bf16[64,1024]{1,0:T(8,128)(2,1)S(1)} collective-permute-done((bf16[64,1024]{1,0:T(8,128)(2,1)}, bf16[64,1024]{1,0:T(8,128)(2,1)S(1)}, u32[]{:S(2)}, u32[]{:S(2)}) %collective-permute-start.11) | collective-permute-done | bytes 131104 | tf_op jit(solution)/shard_map/ppermute | solution.py:95
  86.9 7.0 collective-permute-start.12
  93.9 6.2 collective-permute-done.12
  160.2 11.6 %collective-permute-done.31 = bf16[128,2048]{1,0:T(8,128)(2,1)} collective-permute-done((bf16[128,2048]{1,0:T(8,128)(2,1)}, bf16[128,2048]{1,0:T(8,128)(2,1)}, u32[]{:S(2)}, u32[]{:S(2)}) %collective-permute-start.31) | collective-permute-done | bytes 524320 | tf_op jit(solution)/shard_map/ppermute | solution.py:89
  171.8 10.6 %collective-permute-done.32 = bf16[128,2048]{1,0:T(8,128)(2,1)} collective-permute-done((bf16[128,2048]{1,0:T(8,128)(2,1)S(1)}, bf16[128,2048]{1,0:T(8,128)(2,1)}, u32[]{:S(2)}, u32[]{:S(2)}) %collective-permute-start.32) | collective-permute-done | bytes 524320 | tf_op jit(solution)/shard_map/ppermute | solution.py:89
  188.7 16.4 %collective-permute-start.34 = (f32[12,512]{1,0:T(8,128)S(1)}, f32[12,512]{1,0:T(8,128)S(1)}, u32[]{:S(2)}, u32[]{:S(2)}) collective-permute-start(f32[12,512]{1,0:T(8,128)S(1)} %pad_maximum_fusion.12), channel_id=1, source_target_pairs={{0,8},{4,12},{8,16},{12,20},{16,24},{20,28},{24,0},{28,4},{1,9},{5... | collective-permute-start | bytes 73736 | tf_op jit(solution)/shard_map/ppermute | solution.py:95
  208.8 8.5 copy.204
  217.3 8.4 copy.205
  225.7 10.8 %fusion.3.weight_ref = bf16[4,2048,768]{2,1,0:T(8,128)(2,1)} fusion(bf16[4,2048,352]{2,1,0:T(8,128)(2,1)} %copy.205, bf16[4,2048,352]{2,1,0:T(8,128)(2,1)} %copy.204), kind=kLoop, calls=%fused_computation.6 | loop fusion | flops 50331648 | bytes 24117248 | tf_op jit(solution)/shard_map/concatenate | solution.py:541
  248.7 19.9 %fetch_rows.3 = bf16[4,1152,2048]{2,1,0:T(8,128)(2,1)} custom-call(s32[8,576,1]{2,1,0:T(8,128)} %sub.242.token_ref, bf16[8,512,2048]{2,1,0:T(8,128)(2,1)} %bitcast.328), custom_call_target="tpu_custom_call" | custom-call | flops 9663676416 | bytes 35651584 | tf_op jit(solution)/shard_map/fetch_rows/pallas_call | solution.py:243
  268.6 17.3 %fusion.117.grad_ref = f32[4,1152,352]{2,1,0:T(8,128)} fusion(bf16[4,1152,2048]{2,1,0:T(8,128)(2,1)} %fetch_rows.3, bf16[4,352,2048]{2,1,0:T(8,128)(2,1)} %param.34), kind=kOutput, calls=%fused_computation.354 | convolution fusion | flops 6643777536 | bytes 31129600 | tf_op jit(solution)/shard_map/erd,efd->erf/dot_general | solution.py:545
  285.9 29.4 %all-gather.7.cloned.1.call-done = bf16[4096,2048]{1,0:T(8,128)(2,1)} async-done(((bf16[128,2048]{1,0:T(8,128)(2,1)}), bf16[4096,2048]{1,0:T(8,128)(2,1)}) %all-gather.7.cloned.1.call-update) | async-done | bytes 16777232 | tf_op jit(solution)/shard_map/all_gather | solution.py:517
  315.4 19.2 %fetch_rows.2.rows_ref = bf16[4,1152,2048]{2,1,0:T(8,128)(2,1)} custom-call(s32[8,576,1]{2,1,0:T(8,128)} %sub.242.token_ref, bf16[8,512,2048]{2,1,0:T(8,128)(2,1)} %bitcast.329), custom_call_target="tpu_custom_call" | custom-call | flops 9663676416 | bytes 35651584 | tf_op jit(solution)/shard_map/fetch_rows/pallas_call | solution.py:243
  334.6 43.5 %expert_pass.1 = (bf16[4,1152,2048]{2,1,0:T(8,128)(2,1)}, bf16[4,1152,352]{2,1,0:T(8,128)(2,1)}, bf16[4,1152,352]{2,1,0:T(8,128)(2,1)}, bf16[4,1152,352]{2,1,0:T(8,128)(2,1)}, bf16[4,1152,352]{2,1,0:T(8,128)(2,1)}) custom-call(bf16[4,1152,2048]{2,1,0:T(8,128)(2,1)} %fetch_rows.2.rows_ref, f32[4,1152,352]{2,1,0:T(8,128)} %fusion.117.grad_ref, ...), custom_call_target="tpu_custom_call" | custom-call | flops 26575110144 | bytes 49283072 | tf_op jit(solution)/shard_map/expert_pass/pallas_call | solution.py:351
  378.1 11.2 %return_rows.4 = (bf16[4,128,1024]{2,1,0:T(8,128)(2,1)}, bf16[4,128,1024]{2,1,0:T(8,128)(2,1)}, bf16[4,128,1024]{2,1,0:T(8,128)(2,1)}, bf16[4,128,1024]{2,1,0:T(...) custom-call(s32[4]{0:T(128)} %add_subtract_fusion.order_ref, ...), custom_call_target="tpu_custom_call" | custom-call | flops 4831838208 | bytes 26214400 | tf_op jit(solution)/shard_map/return_rows/pallas_call | solution.py:292
  390.6 15.4 %fusion.119 = f32[4,2048,352]{1,2,0:T(8,128)} fusion(bf16[4,1152,2048]{2,1,0:T(8,128)(2,1)} %fetch_rows.2.rows_ref, bf16[4,1152,352]{2,1,0:T(8,128)(2,1)} %get-tuple-element.108), kind=kOutput, calls=%fused_computation.356 | convolution fusion | flops 6643777536 | bytes 33652736 | tf_op jit(solution)/shard_map/erd,erf->edf/dot_general | solution.py:570
  406.0 17.1 %fusion.rows_ref = bf16[4,1152,2048]{2,1,0:T(8,128)(2,1)} fusion(bf16[4,1152,352]{2,1,0:T(8,128)(2,1)} %get-tuple-element.76, bf16[4,352,2048]{2,1,0:T(8,128)(2,1)} %param.34, f32[4,1152]{1,0:T(4,128)S(1)} %mul.453), kind=kOutput, calls=%fused_computation.1 | convolution fusion | flops 6662651904 | bytes 27904000 | tf_op jit(solution)/shard_map/erf,efd->erd/dot_general | solution.py:562
  423.0 15.1 %fusion.120 = f32[4,2048,352]{1,2,0:T(8,128)} fusion(bf16[4,1152,2048]{2,1,0:T(8,128)(2,1)} %fetch_rows.2.rows_ref, bf16[4,1152,352]{2,1,0:T(8,128)(2,1)} %get-tuple-element.109), kind=kOutput, calls=%fused_computation.357 | convolution fusion | flops 6643777536 | bytes 33652736 | tf_op jit(solution)/shard_map/erd,erf->edf/dot_general | solution.py:573
  438.2 15.4 %fusion.118 = f32[4,352,2048]{2,1,0:T(8,128)} fusion(bf16[4,1152,352]{2,1,0:T(8,128)(2,1)} %get-tuple-element.107, bf16[4,1152,2048]{2,1,0:T(8,128)(2,1)} %fetch_rows.3), kind=kOutput, calls=%fused_computation.355 | convolution fusion | flops 6643777536 | bytes 33652736 | tf_op jit(solution)/shard_map/erf,erd->efd/dot_general | solution.py:567
  453.5 11.1 %return_rows.5 = (bf16[4,128,1024]{2,1,0:T(8,128)(2,1)}, bf16[4,128,1024]{2,1,0:T(8,128)(2,1)}, bf16[4,128,1024]{2,1,0:T(8,128)(2,1)}, bf16[4,128,1024]{2,1,0:T(...) custom-call(s32[4]{0:T(128)} %add_subtract_fusion.order_ref, ...), custom_call_target="tpu_custom_call" | custom-call | flops 4831838208 | bytes 26214400 | tf_op jit(solution)/shard_map/return_rows/pallas_call | solution.py:292
  464.6 8.5 fusion.15
  474.3 6.1 multiply_convert_fusion.3
  485.7 13.3 %return_rows.7 = (bf16[4,128,1024]{2,1,0:T(8,128)(2,1)}, bf16[4,128,1024]{2,1,0:T(8,128)(2,1)}, bf16[4,128,1024]{2,1,0:T(8,128)(2,1)}, bf16[4,128,1024]{2,1,0:T(...) custom-call(s32[4]{0:T(128)} %broadcast_add_fusion.1.order_ref, ...), custom_call_target="tpu_custom_call" | custom-call | flops 4831838208 | bytes 26214400 | tf_op jit(solution)/shard_map/return_rows/pallas_call | solution.py:292
  500.2 6.7 convolution_convert_fusion.6
  508.2 7.7 convolution_convert_fusion
  538.4 13.8 %return_rows.6 = (bf16[4,128,1024]{2,1,0:T(8,128)(2,1)}, bf16[4,128,1024]{2,1,0:T(8,128)(2,1)}, bf16[4,128,1024]{2,1,0:T(8,128)(2,1)}, bf16[4,128,1024]{2,1,0:T(...) custom-call(s32[4]{0:T(128)} %broadcast_add_fusion.1.order_ref, ...), custom_call_target="tpu_custom_call" | custom-call | flops 4831838208 | bytes 26214400 | tf_op jit(solution)/shard_map/return_rows/pallas_call | solution.py:292
  560.6 19.3 %collective-permute-done.77 = bf16[4,128,1024]{2,1,0:T(8,128)(2,1)} collective-permute-done((bf16[4,128,1024]{2,1,0:T(8,128)(2,1)}, bf16[4,128,1024]{2,1,0:T(8,128)(2,1)}, u32[]{:S(2)}, u32[]{:S(2)}) %collective-permute-start.77) | collective-permute-done | bytes 1048608 | tf_op jit(solution)/shard_map/ppermute | solution.py:152
  594.1 9.7 %collective-permute-done.79 = bf16[128,1024]{1,0:T(8,128)(2,1)S(1)} collective-permute-done((bf16[128,1024]{1,0:T(8,128)(2,1)S(1)}, bf16[128,1024]{1,0:T(8,128)(2,1)S(1)}, u32[]{:S(2)}, u32[]{:S(2)}) %collective-permute-start.79) | collective-permute-done | bytes 262176 | tf_op jit(solution)/shard_map/ppermute | solution.py:95
  605.3 6.4 collective-permute-start.85
  615.2 9.2 collective-permute-done.85
  631.8 11.1 %collective-permute-done.87 = bf16[128,2048]{1,0:T(8,128)(2,1)S(1)} collective-permute-done((bf16[128,2048]{1,0:T(8,128)(2,1)S(1)}, bf16[128,2048]{1,0:T(8,128)(2,1)S(1)}, u32[]{:S(2)}, u32[]{:S(2)}) %collective-permute-start.87) | collective-permute-done | bytes 524320 | tf_op jit(solution)/shard_map/ppermute | solution.py:89
  643.0 6.6 collective-permute-done.88
  661.4 19.9 %collective-permute-done.50 = bf16[4,128,1024]{2,1,0:T(8,128)(2,1)} collective-permute-done((bf16[4,128,1024]{2,1,0:T(8,128)(2,1)}, bf16[4,128,1024]{2,1,0:T(8,128)(2,1)}, u32[]{:S(2)}, u32[]{:S(2)}) %collective-permute-start.50) | collective-permute-done | bytes 1048608 | tf_op jit(solution)/shard_map/ppermute | solution.py:159
  718.5 6.5 collective-permute-done.103
  725.7 10.2 %collective-permute-done.104 = bf16[8,64,576]{2,1,0:T(8,128)(2,1)S(1)} collective-permute-done((bf16[8,64,576]{2,1,0:T(8,128)(2,1)S(1)}, bf16[8,64,576]{2,1,0:T(8,128)(2,1)S(1)}, u32[]{:S(2)}, u32[]{:S(2)}) %collective-permute-start.104) | collective-permute-done | bytes 589856 | tf_op jit(solution)/shard_map/ppermute | solution.py:89
  745.9 11.7 %collective-permute-done.51 = bf16[4,128,1024]{2,1,0:T(8,128)(2,1)} collective-permute-done((bf16[4,128,1024]{2,1,0:T(8,128)(2,1)}, bf16[4,128,1024]{2,1,0:T(8,128)(2,1)}, u32[]{:S(2)}, u32[]{:S(2)}) %collective-permute-start.51) | collective-permute-done | bytes 1048608 | tf_op jit(solution)/shard_map/ppermute | solution.py:152
  759.0 7.8 collective-permute-start.52
  779.8 9.1 collective-permute-start.60
  799.1 12.3 %collective-permute-done.58 = bf16[128,1024]{1,0:T(8,128)(2,1)S(1)} collective-permute-done((bf16[128,1024]{1,0:T(8,128)(2,1)S(1)}, bf16[128,1024]{1,0:T(8,128)(2,1)S(1)}, u32[]{:S(2)}, u32[]{:S(2)}) %collective-permute-start.58) | collective-permute-done | bytes 262176 | tf_op jit(solution)/shard_map/ppermute | solution.py:95
  811.3 22.6 %collective-permute-done.59 = bf16[128,1024]{1,0:T(8,128)(2,1)S(1)} collective-permute-done((bf16[128,1024]{1,0:T(8,128)(2,1)S(1)}, bf16[128,1024]{1,0:T(8,128)(2,1)S(1)}, u32[]{:S(2)}, u32[]{:S(2)}) %collective-permute-start.59) | collective-permute-done | bytes 262176 | tf_op jit(solution)/shard_map/ppermute | solution.py:95
  855.3 9.7 %collective-permute-done.62 = bf16[128,2048]{1,0:T(8,128)(2,1)S(1)} collective-permute-done((bf16[128,2048]{1,0:T(8,128)(2,1)}, bf16[128,2048]{1,0:T(8,128)(2,1)S(1)}, u32[]{:S(2)}, u32[]{:S(2)}) %collective-permute-start.62) | collective-permute-done | bytes 524320 | tf_op jit(solution)/shard_map/ppermute | solution.py:89
  865.8 10.4 %collective-permute-done.90 = bf16[128,2048]{1,0:T(8,128)(2,1)S(1)} collective-permute-done((bf16[128,2048]{1,0:T(8,128)(2,1)}, bf16[128,2048]{1,0:T(8,128)(2,1)S(1)}, u32[]{:S(2)}, u32[]{:S(2)}) %collective-permute-start.90) | collective-permute-done | bytes 524320 | tf_op jit(solution)/shard_map/ppermute | solution.py:89
  876.2 9.0 collective-permute-done.91
  902.3 6.1 collective-permute-done.97
  910.9 8.7 collective-permute-done.94
  927.7 13.3 %collective-permute-start.100 = (f32[144]{0:T(256)S(1)}, f32[144]{0:T(256)S(1)}, u32[]{:S(2)}, u32[]{:S(2)}) collective-permute-start(f32[144]{0:T(256)S(1)} %bitcast.379), channel_id=1, source_target_pairs={{0,8},{4,12},{8,16},{12,20},{16,24},{20,28},{24,0},{28,4},{1,9},{5... | collective-permute-start | bytes 1736 | tf_op jit(solution)/shard_map/ppermute | solution.py:95
  (613 shorter events, 338.1 us)
Async XLA Ops:
  7.2 177.1 %all-gather.5.cloned.1.call-start = ((), (), s32[]{:S(2)}) async-start(), calls=%async_computation.4 | async-start | bytes 17301504 | tf_op jit(solution)/shard_map/all_gather | solution.py:450
  22.1 293.2 %all-gather.7.cloned.1.call-start = ((), (), s32[]{:S(2)}) async-start(), calls=%async_computation.5 | async-start | bytes 17301504 | tf_op jit(solution)/shard_map/all_gather | solution.py:517
  22.2 83.4 %collective-permute-start.17 = (bf16[256,768]{1,0:T(8,128)(2,1)}, bf16[256,768]{1,0:T(8,128)(2,1)}, u32[]{:S(2)}, u32[]{:S(2)}) collective-permute-start(bf16[256,768]{1,0:T(8,128)(2,1)} %param.23), channel_id=1, source_target_pairs={{0,8},{4,12},{8,16},{12,20},{16,24},{20,28},{24,0},{28,4},{1,9},{5... | collective-permute-start | bytes 1179656 | tf_op jit(solution)/shard_map/ppermute | solution.py:95
  24.2 81.5 %collective-permute-start.18 = (bf16[256,768]{1,0:T(8,128)(2,1)}, bf16[256,768]{1,0:T(8,128)(2,1)}, u32[]{:S(2)}, u32[]{:S(2)}) collective-permute-start(bf16[256,768]{1,0:T(8,128)(2,1)} %param.23), channel_id=1, source_target_pairs={{0,16},{4,20},{8,24},{12,28},{16,0},{20,4},{24,8},{28,12},{1,17},{... | collective-permute-start | bytes 1179656 | tf_op jit(solution)/shard_map/ppermute | solution.py:95
  28.9 33.6 %collective-permute-start.8 = (bf16[8,64,579]{2,1,0:T(8,128)(2,1)S(1)}, bf16[8,64,579]{2,1,0:T(8,128)(2,1)S(1)}, u32[]{:S(2)}, u32[]{:S(2)}) collective-permute-start(bf16[8,64,579]{2,1,0:T(8,128)(2,1)S(1)} %bitcast_dynamic-update-slice_fusion.40), channel_id=1, source_target_pairs={{0,2},{1,3},{2,0},{3,1},{4,6},{5,7},{6,4},{7,5},{8,10},{9,11},{10,... | collective-permute-start | bytes 1778696 | tf_op jit(solution)/shard_map/ppermute | solution.py:89
  30.9 31.8 %collective-permute-start.9 = (bf16[8,64,579]{2,1,0:T(8,128)(2,1)S(1)}, bf16[8,64,579]{2,1,0:T(8,128)(2,1)S(1)}, u32[]{:S(2)}, u32[]{:S(2)}) collective-permute-start(bf16[8,64,579]{2,1,0:T(8,128)(2,1)S(1)} %bitcast_dynamic-update-slice_fusion.40), channel_id=1, source_target_pairs={{0,3},{1,0},{2,1},{3,2},{4,7},{5,4},{6,5},{7,6},{8,11},{9,8},{10,9... | collective-permute-start | bytes 1778696 | tf_op jit(solution)/shard_map/ppermute | solution.py:89
  49.7 56.4 %collective-permute-start.19 = (bf16[256,768]{1,0:T(8,128)(2,1)}, bf16[256,768]{1,0:T(8,128)(2,1)}, u32[]{:S(2)}, u32[]{:S(2)}) collective-permute-start(bf16[256,768]{1,0:T(8,128)(2,1)} %param.23), channel_id=1, source_target_pairs={{0,24},{4,28},{8,0},{12,4},{16,8},{20,12},{24,16},{28,20},{1,25},{... | collective-permute-start | bytes 1179656 | tf_op jit(solution)/shard_map/ppermute | solution.py:95
  62.5 54.1 %collective-permute-start.20 = (bf16[256,768]{1,0:T(8,128)(2,1)}, bf16[256,768]{1,0:T(8,128)(2,1)}, u32[]{:S(2)}, u32[]{:S(2)}) collective-permute-start(bf16[256,768]{1,0:T(8,128)(2,1)} %param.23), channel_id=1, source_target_pairs={{0,4},{4,0},{8,12},{12,8},{16,20},{20,16},{24,28},{28,24},{1,5},{5... | collective-permute-start | bytes 1179656 | tf_op jit(solution)/shard_map/ppermute | solution.py:99
  106.5 34.6 %collective-permute-start.24 = (bf16[512,256]{0,1:T(8,128)(2,1)}, bf16[512,256]{0,1:T(8,128)(2,1)}, u32[]{:S(2)}, u32[]{:S(2)}) collective-permute-start(bf16[512,256]{0,1:T(8,128)(2,1)} %copy.191), channel_id=1, source_target_pairs={{0,8},{4,12},{8,16},{12,20},{16,24},{20,28},{24,0},{28,4},{1,9},{5... | collective-permute-start | bytes 786440 | tf_op jit(solution)/shard_map/ppermute | solution.py:95
  116.7 29.7 %collective-permute-start.25 = (bf16[512,256]{0,1:T(8,128)(2,1)}, bf16[512,256]{0,1:T(8,128)(2,1)}, u32[]{:S(2)}, u32[]{:S(2)}) collective-permute-start(bf16[512,256]{0,1:T(8,128)(2,1)} %copy.191), channel_id=1, source_target_pairs={{0,16},{4,20},{8,24},{12,28},{16,0},{20,4},{24,8},{28,12},{1,17},{... | collective-permute-start | bytes 786440 | tf_op jit(solution)/shard_map/ppermute | solution.py:95
  187.6 277.0 %all-gather.9.cloned.1.call-start = ((), (), s32[]{:S(2)}) async-start(), calls=%async_computation.6 | async-start | bytes 6488064 | tf_op jit(solution)/shard_map/all_gather | solution.py:520
  188.6 285.6 %all-gather.11.cloned.1.call-start = ((), (), s32[]{:S(2)}) async-start(), calls=%async_computation.7 | async-start | bytes 3244032 | tf_op jit(solution)/shard_map/all_gather | solution.py:523
  188.7 48.3 %collective-permute-start.34 = (f32[12,512]{1,0:T(8,128)S(1)}, f32[12,512]{1,0:T(8,128)S(1)}, u32[]{:S(2)}, u32[]{:S(2)}) collective-permute-start(f32[12,512]{1,0:T(8,128)S(1)} %pad_maximum_fusion.12), channel_id=1, source_target_pairs={{0,8},{4,12},{8,16},{12,20},{16,24},{20,28},{24,0},{28,4},{1,9},{5... | collective-permute-start | bytes 73736 | tf_op jit(solution)/shard_map/ppermute | solution.py:95
  205.1 32.4 %collective-permute-start.35 = (f32[12,512]{1,0:T(8,128)S(1)}, f32[12,512]{1,0:T(8,128)S(1)}, u32[]{:S(2)}, u32[]{:S(2)}) collective-permute-start(f32[12,512]{1,0:T(8,128)S(1)} %pad_maximum_fusion.12), channel_id=1, source_target_pairs={{0,16},{4,20},{8,24},{12,28},{16,0},{20,4},{24,8},{28,12},{1,17},{... | collective-permute-start | bytes 73736 | tf_op jit(solution)/shard_map/ppermute | solution.py:95
  205.1 32.5 %collective-permute-start.36 = (f32[12,512]{1,0:T(8,128)S(1)}, f32[12,512]{1,0:T(8,128)S(1)}, u32[]{:S(2)}, u32[]{:S(2)}) collective-permute-start(f32[12,512]{1,0:T(8,128)S(1)} %pad_maximum_fusion.12), channel_id=1, source_target_pairs={{0,24},{4,28},{8,0},{12,4},{16,8},{20,12},{24,16},{28,20},{1,25},{... | collective-permute-start | bytes 73736 | tf_op jit(solution)/shard_map/ppermute | solution.py:95
  207.6 30.8 %collective-permute-start.37 = (f32[12,512]{1,0:T(8,128)S(1)}, f32[12,512]{1,0:T(8,128)S(1)}, u32[]{:S(2)}, u32[]{:S(2)}) collective-permute-start(f32[12,512]{1,0:T(8,128)S(1)} %pad_maximum_fusion.12), channel_id=1, source_target_pairs={{0,4},{4,0},{8,12},{12,8},{16,20},{20,16},{24,28},{28,24},{1,5},{5... | collective-permute-start | bytes 73736 | tf_op jit(solution)/shard_map/ppermute | solution.py:99
  207.6 715.1 %reduce-scatter.7.cloned.1.call-start = ((), (), s32[]{:S(2)}) async-start(), calls=%async_computation.9 | async-start | bytes 3244032 | tf_op jit(solution)/shard_map/reduce_scatter | solution.py:674
  389.3 83.7 %collective-permute-start.67 = (bf16[4,128,1024]{2,1,0:T(8,128)(2,1)}, bf16[4,128,1024]{2,1,0:T(8,128)(2,1)S(1)}, u32[]{:S(2)}, u32[]{:S(2)}) collective-permute-start(bf16[4,128,1024]{2,1,0:T(8,128)(2,1)} %get-tuple-element.75), channel_id=1, source_target_pairs={{0,4},{4,0},{8,12},{12,8},{16,20},{20,16},{24,28},{28,24},{1,5},{5... | collective-permute-start | bytes 3145736 | tf_op jit(solution)/shard_map/ppermute | solution.py:99
  389.6 83.7 %collective-permute-start.68 = (bf16[4,128,1024]{2,1,0:T(8,128)(2,1)}, bf16[4,128,1024]{2,1,0:T(8,128)(2,1)}, u32[]{:S(2)}, u32[]{:S(2)}) collective-permute-start(bf16[4,128,1024]{2,1,0:T(8,128)(2,1)} %get-tuple-element.93), channel_id=1, source_target_pairs={{0,4},{4,0},{8,12},{12,8},{16,20},{20,16},{24,28},{28,24},{1,5},{5... | collective-permute-start | bytes 3145736 | tf_op jit(solution)/shard_map/ppermute | solution.py:99
  389.8 83.7 %collective-permute-start.69 = (bf16[4,128,1024]{2,1,0:T(8,128)(2,1)}, bf16[4,128,1024]{2,1,0:T(8,128)(2,1)}, u32[]{:S(2)}, u32[]{:S(2)}) collective-permute-start(bf16[4,128,1024]{2,1,0:T(8,128)(2,1)} %get-tuple-element.94), channel_id=1, source_target_pairs={{0,4},{4,0},{8,12},{12,8},{16,20},{20,16},{24,28},{28,24},{1,5},{5... | collective-permute-start | bytes 3145736 | tf_op jit(solution)/shard_map/ppermute | solution.py:99
  390.1 83.7 %collective-permute-start.70 = (bf16[4,128,1024]{2,1,0:T(8,128)(2,1)}, bf16[4,128,1024]{2,1,0:T(8,128)(2,1)}, u32[]{:S(2)}, u32[]{:S(2)}) collective-permute-start(bf16[4,128,1024]{2,1,0:T(8,128)(2,1)} %get-tuple-element.95), channel_id=1, source_target_pairs={{0,4},{4,0},{8,12},{12,8},{16,20},{20,16},{24,28},{28,24},{1,5},{5... | collective-permute-start | bytes 3145736 | tf_op jit(solution)/shard_map/ppermute | solution.py:99
  390.4 94.2 %collective-permute-start.71 = (bf16[4,128,1024]{2,1,0:T(8,128)(2,1)}, bf16[4,128,1024]{2,1,0:T(8,128)(2,1)}, u32[]{:S(2)}, u32[]{:S(2)}) collective-permute-start(bf16[4,128,1024]{2,1,0:T(8,128)(2,1)} %get-tuple-element.96), channel_id=1, source_target_pairs={{0,4},{4,0},{8,12},{12,8},{16,20},{20,16},{24,28},{28,24},{1,5},{5... | collective-permute-start | bytes 3145736 | tf_op jit(solution)/shard_map/ppermute | solution.py:99
  484.6 440.0 %reduce-scatter.9.cloned.1.call-start = ((), (), s32[]{:S(2)}) async-start(), calls=%async_computation.10 | async-start | bytes 2359296 | tf_op jit(solution)/shard_map/reduce_scatter | solution.py:677
  485.0 30.9 %collective-permute-start.43 = (bf16[4,128,1024]{2,1,0:T(8,128)(2,1)}, bf16[4,128,1024]{2,1,0:T(8,128)(2,1)}, u32[]{:S(2)}, u32[]{:S(2)}) collective-permute-start(bf16[4,128,1024]{2,1,0:T(8,128)(2,1)} %get-tuple-element.79), channel_id=1, source_target_pairs={{0,4},{4,0},{8,12},{12,8},{16,20},{20,16},{24,28},{28,24},{1,5},{5... | collective-permute-start | bytes 3145736 | tf_op jit(solution)/shard_map/ppermute | solution.py:99
  485.2 30.8 %collective-permute-start.44 = (bf16[4,128,1024]{2,1,0:T(8,128)(2,1)}, bf16[4,128,1024]{2,1,0:T(8,128)(2,1)}, u32[]{:S(2)}, u32[]{:S(2)}) collective-permute-start(bf16[4,128,1024]{2,1,0:T(8,128)(2,1)} %get-tuple-element.80), channel_id=1, source_target_pairs={{0,4},{4,0},{8,12},{12,8},{16,20},{20,16},{24,28},{28,24},{1,5},{5... | collective-permute-start | bytes 3145736 | tf_op jit(solution)/shard_map/ppermute | solution.py:99
  485.5 30.9 %collective-permute-start.45 = (bf16[4,128,1024]{2,1,0:T(8,128)(2,1)}, bf16[4,128,1024]{2,1,0:T(8,128)(2,1)}, u32[]{:S(2)}, u32[]{:S(2)}) collective-permute-start(bf16[4,128,1024]{2,1,0:T(8,128)(2,1)} %get-tuple-element.81), channel_id=1, source_target_pairs={{0,4},{4,0},{8,12},{12,8},{16,20},{20,16},{24,28},{28,24},{1,5},{5... | collective-permute-start | bytes 3145736 | tf_op jit(solution)/shard_map/ppermute | solution.py:99
  524.9 27.4 %collective-permute-start.75 = (bf16[4,128,1024]{2,1,0:T(8,128)(2,1)}, bf16[4,128,1024]{2,1,0:T(8,128)(2,1)}, u32[]{:S(2)}, u32[]{:S(2)}) collective-permute-start(bf16[4,128,1024]{2,1,0:T(8,128)(2,1)} %get-tuple-element.102), channel_id=1, source_target_pairs={{0,1},{1,0},{2,3},{3,2},{4,5},{5,4},{6,7},{7,6},{8,9},{9,8},{10,11... | collective-permute-start | bytes 3145736 | tf_op jit(solution)/shard_map/ppermute | solution.py:159
  536.6 43.3 %collective-permute-start.77 = (bf16[4,128,1024]{2,1,0:T(8,128)(2,1)}, bf16[4,128,1024]{2,1,0:T(8,128)(2,1)}, u32[]{:S(2)}, u32[]{:S(2)}) collective-permute-start(bf16[4,128,1024]{2,1,0:T(8,128)(2,1)} %add_convert_fusion.3), channel_id=1, source_target_pairs={{0,2},{1,3},{2,0},{3,1},{4,6},{5,7},{6,4},{7,5},{8,10},{9,11},{10,... | collective-permute-start | bytes 3145736 | tf_op jit(solution)/shard_map/ppermute | solution.py:152
  537.3 48.1 %collective-permute-start.83 = (bf16[4,128,1024]{2,1,0:T(8,128)(2,1)}, bf16[4,128,1024]{2,1,0:T(8,128)(2,1)}, u32[]{:S(2)}, u32[]{:S(2)}) collective-permute-start(bf16[4,128,1024]{2,1,0:T(8,128)(2,1)} %add_convert_fusion.1), channel_id=1, source_target_pairs={{0,1},{1,0},{2,3},{3,2},{4,5},{5,4},{6,7},{7,6},{8,9},{9,8},{10,11... | collective-permute-start | bytes 3145736 | tf_op jit(solution)/shard_map/ppermute | solution.py:159
  587.6 37.0 %collective-permute-start.64 = (bf16[128,2048]{1,0:T(8,128)(2,1)S(1)}, bf16[128,2048]{1,0:T(8,128)(2,1)S(1)}, u32[]{:S(2)}, u32[]{:S(2)}) collective-permute-start(bf16[128,2048]{1,0:T(8,128)(2,1)S(1)} %get-tuple-element.224), channel_id=1, source_target_pairs={{0,1},{1,2},{2,3},{3,0},{4,5},{5,6},{6,7},{7,4},{8,9},{9,10},{10,1... | collective-permute-start | bytes 1572872 | tf_op jit(solution)/shard_map/ppermute | solution.py:89
  592.6 32.1 %collective-permute-start.65 = (bf16[128,2048]{1,0:T(8,128)(2,1)S(1)}, bf16[128,2048]{1,0:T(8,128)(2,1)S(1)}, u32[]{:S(2)}, u32[]{:S(2)}) collective-permute-start(bf16[128,2048]{1,0:T(8,128)(2,1)S(1)} %get-tuple-element.226), channel_id=1, source_target_pairs={{0,2},{1,3},{2,0},{3,1},{4,6},{5,7},{6,4},{7,5},{8,10},{9,11},{10,... | collective-permute-start | bytes 1572872 | tf_op jit(solution)/shard_map/ppermute | solution.py:89
  653.9 272.5 %reduce-scatter.5.cloned.1.call-start = ((), (), s32[]{:S(2)}) async-start(), calls=%async_computation.8 | async-start | bytes 6488064 | tf_op jit(solution)/shard_map/reduce_scatter | solution.py:669
  654.6 296.3 %reduce-scatter.11.cloned.1.call-start = ((), (), s32[]{:S(2)}) async-start(), calls=%async_computation.11 | async-start | bytes 5455872 | tf_op jit(solution)/shard_map/reduce_scatter | solution.py:700
  656.7 27.3 %collective-permute-start.56 = (bf16[4,128,1024]{2,1,0:T(8,128)(2,1)}, bf16[4,128,1024]{2,1,0:T(8,128)(2,1)}, u32[]{:S(2)}, u32[]{:S(2)}) collective-permute-start(bf16[4,128,1024]{2,1,0:T(8,128)(2,1)} %get-tuple-element.92), channel_id=1, source_target_pairs={{0,2},{1,3},{2,0},{3,1},{4,6},{5,7},{6,4},{7,5},{8,10},{9,11},{10,... | collective-permute-start | bytes 3145736 | tf_op jit(solution)/shard_map/ppermute | solution.py:152
  659.6 83.6 %collective-permute-start.49 = (bf16[4,128,1024]{2,1,0:T(8,128)(2,1)}, bf16[4,128,1024]{2,1,0:T(8,128)(2,1)}, u32[]{:S(2)}, u32[]{:S(2)}) collective-permute-start(bf16[4,128,1024]{2,1,0:T(8,128)(2,1)} %get-tuple-element.86), channel_id=1, source_target_pairs={{0,1},{1,0},{2,3},{3,2},{4,5},{5,4},{6,7},{7,6},{8,9},{9,8},{10,11... | collective-permute-start | bytes 3145736 | tf_op jit(solution)/shard_map/ppermute | solution.py:159
  660.1 110.2 %collective-permute-start.55 = (bf16[4,128,1024]{2,1,0:T(8,128)(2,1)}, bf16[4,128,1024]{2,1,0:T(8,128)(2,1)}, u32[]{:S(2)}, u32[]{:S(2)}) collective-permute-start(bf16[4,128,1024]{2,1,0:T(8,128)(2,1)} %get-tuple-element.90), channel_id=1, source_target_pairs={{0,2},{1,3},{2,0},{3,1},{4,6},{5,7},{6,4},{7,5},{8,10},{9,11},{10,... | collective-permute-start | bytes 3145736 | tf_op jit(solution)/shard_map/ppermute | solution.py:152
  708.3 27.6 %collective-permute-start.104 = (bf16[8,64,576]{2,1,0:T(8,128)(2,1)S(1)}, bf16[8,64,576]{2,1,0:T(8,128)(2,1)S(1)}, u32[]{:S(2)}, u32[]{:S(2)}) collective-permute-start(bf16[8,64,576]{2,1,0:T(8,128)(2,1)S(1)} %get-tuple-element.219), channel_id=1, source_target_pairs={{0,2},{1,3},{2,0},{3,1},{4,6},{5,7},{6,4},{7,5},{8,10},{9,11},{10,... | collective-permute-start | bytes 1769480 | tf_op jit(solution)/shard_map/ppermute | solution.py:89
  708.8 31.6 %collective-permute-start.105 = (bf16[8,64,576]{2,1,0:T(8,128)(2,1)S(1)}, bf16[8,64,576]{2,1,0:T(8,128)(2,1)S(1)}, u32[]{:S(2)}, u32[]{:S(2)}) collective-permute-start(bf16[8,64,576]{2,1,0:T(8,128)(2,1)S(1)} %get-tuple-element.218), channel_id=1, source_target_pairs={{0,3},{1,0},{2,1},{3,2},{4,7},{5,4},{6,5},{7,6},{8,11},{9,8},{10,9... | collective-permute-start | bytes 1769480 | tf_op jit(solution)/shard_map/ppermute | solution.py:89
  725.0 32.6 %collective-permute-start.51 = (bf16[4,128,1024]{2,1,0:T(8,128)(2,1)}, bf16[4,128,1024]{2,1,0:T(8,128)(2,1)}, u32[]{:S(2)}, u32[]{:S(2)}) collective-permute-start(bf16[4,128,1024]{2,1,0:T(8,128)(2,1)} %add_convert_fusion.7), channel_id=1, source_target_pairs={{0,2},{1,3},{2,0},{3,1},{4,6},{5,7},{6,4},{7,5},{8,10},{9,11},{10,... | collective-permute-start | bytes 3145736 | tf_op jit(solution)/shard_map/ppermute | solution.py:152
  735.9 36.0 %collective-permute-start.57 = (bf16[4,128,1024]{2,1,0:T(8,128)(2,1)S(1)}, bf16[4,128,1024]{2,1,0:T(8,128)(2,1)}, u32[]{:S(2)}, u32[]{:S(2)}) collective-permute-start(bf16[4,128,1024]{2,1,0:T(8,128)(2,1)S(1)} %copy-done.41), channel_id=1, source_target_pairs={{0,1},{1,0},{2,3},{3,2},{4,5},{5,4},{6,7},{7,6},{8,9},{9,8},{10,11... | collective-permute-start | bytes 3145736 | tf_op jit(solution)/shard_map/ppermute | solution.py:159
  766.8 27.9 %collective-permute-start.53 = (bf16[128,1024]{1,0:T(8,128)(2,1)S(1)}, bf16[128,1024]{1,0:T(8,128)(2,1)S(1)}, u32[]{:S(2)}, u32[]{:S(2)}) collective-permute-start(bf16[128,1024]{1,0:T(8,128)(2,1)S(1)} %get-tuple-element.237), channel_id=1, source_target_pairs={{0,16},{4,20},{8,24},{12,28},{16,0},{20,4},{24,8},{28,12},{1,17},{... | collective-permute-start | bytes 786440 | tf_op jit(solution)/shard_map/ppermute | solution.py:95
  770.3 27.6 %collective-permute-start.54 = (bf16[128,1024]{1,0:T(8,128)(2,1)S(1)}, bf16[128,1024]{1,0:T(8,128)(2,1)S(1)}, u32[]{:S(2)}, u32[]{:S(2)}) collective-permute-start(bf16[128,1024]{1,0:T(8,128)(2,1)S(1)} %get-tuple-element.236), channel_id=1, source_target_pairs={{0,24},{4,28},{8,0},{12,4},{16,8},{20,12},{24,16},{28,20},{1,25},{... | collective-permute-start | bytes 786440 | tf_op jit(solution)/shard_map/ppermute | solution.py:95
  773.3 38.0 %collective-permute-start.58 = (bf16[128,1024]{1,0:T(8,128)(2,1)S(1)}, bf16[128,1024]{1,0:T(8,128)(2,1)S(1)}, u32[]{:S(2)}, u32[]{:S(2)}) collective-permute-start(bf16[128,1024]{1,0:T(8,128)(2,1)S(1)} %get-tuple-element.238), channel_id=1, source_target_pairs={{0,8},{4,12},{8,16},{12,20},{16,24},{20,28},{24,0},{28,4},{1,9},{5... | collective-permute-start | bytes 786440 | tf_op jit(solution)/shard_map/ppermute | solution.py:95
  775.4 58.5 %collective-permute-start.59 = (bf16[128,1024]{1,0:T(8,128)(2,1)S(1)}, bf16[128,1024]{1,0:T(8,128)(2,1)S(1)}, u32[]{:S(2)}, u32[]{:S(2)}) collective-permute-start(bf16[128,1024]{1,0:T(8,128)(2,1)S(1)} %get-tuple-element.240), channel_id=1, source_target_pairs={{0,16},{4,20},{8,24},{12,28},{16,0},{20,4},{24,8},{28,12},{1,17},{... | collective-permute-start | bytes 786440 | tf_op jit(solution)/shard_map/ppermute | solution.py:95
  779.8 54.1 %collective-permute-start.60 = (bf16[128,1024]{1,0:T(8,128)(2,1)S(1)}, bf16[128,1024]{1,0:T(8,128)(2,1)S(1)}, u32[]{:S(2)}, u32[]{:S(2)}) collective-permute-start(bf16[128,1024]{1,0:T(8,128)(2,1)S(1)} %get-tuple-element.239), channel_id=1, source_target_pairs={{0,24},{4,28},{8,0},{12,4},{16,8},{20,12},{24,16},{28,20},{1,25},{... | collective-permute-start | bytes 786440 | tf_op jit(solution)/shard_map/ppermute | solution.py:95
  839.0 60.2 %collective-permute-start.63 = (bf16[128,2048]{1,0:T(8,128)(2,1)}, bf16[128,2048]{1,0:T(8,128)(2,1)}, u32[]{:S(2)}, u32[]{:S(2)}) collective-permute-start(bf16[128,2048]{1,0:T(8,128)(2,1)} %get-tuple-element.209), channel_id=1, source_target_pairs={{0,3},{1,0},{2,1},{3,2},{4,7},{5,4},{6,5},{7,6},{8,11},{9,8},{10,9... | collective-permute-start | bytes 1572872 | tf_op jit(solution)/shard_map/ppermute | solution.py:89
  850.6 34.6 %collective-permute-start.91 = (bf16[128,2048]{1,0:T(8,128)(2,1)}, bf16[128,2048]{1,0:T(8,128)(2,1)S(1)}, u32[]{:S(2)}, u32[]{:S(2)}) collective-permute-start(bf16[128,2048]{1,0:T(8,128)(2,1)} %get-tuple-element.223), channel_id=1, source_target_pairs={{0,2},{1,3},{2,0},{3,1},{4,6},{5,7},{6,4},{7,5},{8,10},{9,11},{10,... | collective-permute-start | bytes 1572872 | tf_op jit(solution)/shard_map/ppermute | solution.py:89
  853.7 32.4 %collective-permute-start.92 = (bf16[128,2048]{1,0:T(8,128)(2,1)}, bf16[128,2048]{1,0:T(8,128)(2,1)}, u32[]{:S(2)}, u32[]{:S(2)}) collective-permute-start(bf16[128,2048]{1,0:T(8,128)(2,1)} %get-tuple-element.222), channel_id=1, source_target_pairs={{0,3},{1,0},{2,1},{3,2},{4,7},{5,4},{6,5},{7,6},{8,11},{9,8},{10,9... | collective-permute-start | bytes 1572872 | tf_op jit(solution)/shard_map/ppermute | solution.py:89
  (162 other events, 1917.2 us)
Sparse Core Ops, SparseCore 0:
  22.3 160.0 all-gather.4
  187.7 127.5 all-gather.6
  317.5 59.0 all-gather.8
  378.0 35.2 all-gather.10
  484.7 37.3 reduce-scatter.6
  654.0 43.7 reduce-scatter.8
  700.1 63.2 reduce-scatter.4
  765.7 90.3 reduce-scatter.10
